TPU v7x, 512 devices: a whole 4x4x16 slice. The times are simulated.
512 devices in a mesh: expert: 64 (over z, x), ffn: 8 (over y, core).
Axes of the slice: x: 4, y: 4, z: 16, core: 2. Of those that a mesh axis runs over, the one named last changes fastest.
Arguments:
- tokens: bfloat16 [8192, 4096], P('expert'), may hold values from -6 to 6
- cotangent: bfloat16 [8192, 4096], P('expert'), may hold values from -6 to 6
- expert_ids: int32 [8192, 1], P('expert'), may hold values from 0 to 7; in each aligned block of 128 rows (0 to 127, 128 to 255, ...) at most 20 rows name the same one
- in_weight: bfloat16 [64, 512, 5120], P('expert', None, 'ffn'), may hold values from -0.09375 to 0.09375
- out_weight: bfloat16 [64, 5120, 512], P('expert', 'ffn'), may hold values from -0.078125 to 0.078125
- width_states: float32 [2, 8, 4096], replicated, may hold values from 76.8 to 768
- hidden_states: float32 [2, 8, 5120], P(None, None, 'ffn'), may hold values from 76.8 to 768
Outputs:
- update_in: bfloat16 [64, 512, 5120], P('expert', None, 'ffn')
- update_out: bfloat16 [64, 5120, 512], P('expert', 'ffn')
Inputs may be any that keep to these rules, and one draw needn't show every extreme that they name: `expert_ids`: within each block of 128 consecutive rows at most 20 name the same expert; in some block some expert is named by exactly 20 rows; every expert is named somewhere.
All inputs are finite; a program needn't handle non-finite values.
Results may differ from a plain program's by a relative error of at most 0.0049.
Values may be sent and summed in bfloat16 or wider, within the bound.
A program may use at most 64 MiB of HBM per device.

v0:
```python
import math

import jax
import jax.numpy as jnp
from jax import lax
from jax.sharding import PartitionSpec as P

D = 4096
FF = 5120
GROUP = 8


DECAY_RATE = 0.9
EPS_ONE = 1e-30
ROOT_COEF = math.sqrt(2.0 / math.pi)
CUBIC_COEF = 0.044715


def partner_2(value, axis, bit):
    mask = 2**bit
    pairs = [(source, source ^ mask) for source in range(lax.axis_size(axis))]
    return lax.ppermute(value, axis, pairs)


def gelu_pair(inputs):
    inner = ROOT_COEF * (inputs + CUBIC_COEF * inputs * inputs * inputs)
    tangent = jnp.tanh(inner)
    act_value = 0.5 * inputs * (1.0 + tangent)
    act_slope = 0.5 * (1.0 + tangent) + 0.5 * inputs * (1.0 - tangent * tangent) * ROOT_COEF * (
        1.0 + 3.0 * CUBIC_COEF * inputs * inputs
    )
    return (act_value, act_slope)


def group_total(values):
    for section in range(GROUP.bit_length() - 1):
        values = values + partner_2(values, "expert", section)
    return values


def shards(tokens, cotangent, expert_ids, in_weight, out_weight, width_states, hidden_states):
    experts = width_states.shape[1]
    tok_rows = tokens.shape[0]
    capacity = 5 * tok_rows // (4 * experts)
    block_width = tokens.shape[1] // GROUP
    route_ids = expert_ids[:, 0]
    onehot = (route_ids[:, None] == jnp.arange(experts, dtype=jnp.int32)[None, :]).astype(jnp.int32)
    before = jnp.cumsum(onehot, axis=0) - onehot
    slot_index = jnp.sum(before * onehot, axis=1)
    target = slot_index * experts + route_ids
    select = (jnp.arange(capacity * experts, dtype=jnp.int32)[:, None] == target[None, :]).astype(
        jnp.bfloat16
    )
    sent_tokens = (
        jnp.dot(select, tokens, preferred_element_type=jnp.float32)
        .astype(jnp.bfloat16)
        .reshape(capacity, experts * GROUP, block_width)
    )
    sent_cotangent = (
        jnp.dot(select, cotangent, preferred_element_type=jnp.float32)
        .astype(jnp.bfloat16)
        .reshape(capacity, experts * GROUP, block_width)
    )
    got_tokens, got_cotangent = (
        lax.all_to_all(sent_tokens, "expert", split_axis=1, concat_axis=0, tiled=True),
        lax.all_to_all(sent_cotangent, "expert", split_axis=1, concat_axis=0, tiled=True),
    )
    expert_tokens = got_tokens.reshape(-1, block_width)
    expert_cotangent = got_cotangent.reshape(-1, block_width)
    local_in = in_weight[0]
    local_out = out_weight[0]
    pre_partial = jnp.dot(expert_tokens, local_in, preferred_element_type=jnp.float32)
    back_partial = lax.dot_general(
        expert_cotangent, local_out, (((1,), (1,)), ((), ())), preferred_element_type=jnp.float32
    )
    partials = jnp.stack([pre_partial, back_partial])
    position = lax.axis_index("expert")
    levels = GROUP.bit_length() - 1
    for section in range(levels):
        half_rows = partials.shape[1] // 2
        lower = partials[:, :half_rows]
        upper = partials[:, half_rows:]
        upper_side = position >> section & 1 == 1
        kept_rows = jnp.where(upper_side, upper, lower)
        sent_rows = jnp.where(upper_side, lower, upper)
        partials = kept_rows + partner_2(sent_rows, "expert", section)
    for section in reversed(range(levels)):
        partner = partner_2(partials, "expert", section)
        upper_side = position >> section & 1 == 1
        partials = jnp.where(
            upper_side,
            jnp.concatenate([partner, partials], axis=1),
            jnp.concatenate([partials, partner], axis=1),
        )
    act_value, act_slope = gelu_pair(partials[0])
    hidden = act_value.astype(jnp.bfloat16)
    pre_grad = (partials[1] * act_slope).astype(jnp.bfloat16)
    grad_in = lax.dot_general(
        expert_tokens, pre_grad, (((0,), (0,)), ((), ())), preferred_element_type=jnp.float32
    )
    grad_out = lax.dot_general(
        hidden, expert_cotangent, (((0,), (0,)), ((), ())), preferred_element_type=jnp.float32
    )
    expert = position // GROUP
    block_index = position % GROUP
    width_pick = lax.dynamic_index_in_dim(width_states, expert, 1, keepdims=False)
    width_local = lax.dynamic_slice_in_dim(width_pick, block_index * block_width, block_width, 1)
    hidden_local = lax.dynamic_index_in_dim(hidden_states, expert, 1, keepdims=False)
    square_in = grad_in * grad_in + EPS_ONE
    square_out = grad_out * grad_out + EPS_ONE
    pair_sums = group_total(jnp.stack([jnp.sum(square_in, axis=0), jnp.sum(square_out, axis=1)]))
    small_totals = jnp.stack(
        [jnp.sum(pair_sums[0]), jnp.sum(pair_sums[1]), jnp.sum(hidden_local[1])]
    )
    row_in, col_out, totals = lax.psum(
        (jnp.sum(square_in, axis=1), jnp.sum(square_out, axis=0), small_totals), "ffn"
    )
    whole_count = float(D) * float(FF)
    rows_in = DECAY_RATE * width_local[0] + (1.0 - DECAY_RATE) * row_in / FF
    cols_in = DECAY_RATE * hidden_local[0] + (1.0 - DECAY_RATE) * pair_sums[0] / D
    mean_in = DECAY_RATE * jnp.mean(width_pick[0]) + (1.0 - DECAY_RATE) * totals[0] / whole_count
    rows_out = DECAY_RATE * hidden_local[1] + (1.0 - DECAY_RATE) * pair_sums[1] / D
    cols_out = DECAY_RATE * width_local[1] + (1.0 - DECAY_RATE) * col_out / FF
    mean_out = DECAY_RATE * totals[2] / FF + (1.0 - DECAY_RATE) * totals[1] / whole_count
    raw_in = grad_in * lax.rsqrt(rows_in[:, None] * cols_in[None, :] / mean_in)
    raw_out = grad_out * lax.rsqrt(rows_out[:, None] * cols_out[None, :] / mean_out)
    norm_sums = group_total(jnp.stack([jnp.sum(raw_in * raw_in), jnp.sum(raw_out * raw_out)]))
    norm_sums = lax.psum(norm_sums, "ffn")
    clip_ratio = jnp.sqrt(norm_sums / whole_count)
    update_in = (raw_in / jnp.maximum(1.0, clip_ratio[0])).astype(jnp.bfloat16)[None]
    update_out = (raw_out / jnp.maximum(1.0, clip_ratio[1])).astype(jnp.bfloat16)[None]
    return (update_in, update_out)


def solution(mesh):
    return jax.shard_map(
        shards,
        mesh=mesh,
        in_specs=(
            P("expert", None),
            P("expert", None),
            P("expert", None),
            P("expert", None, "ffn"),
            P("expert", "ffn", None),
            P(),
            P(None, None, "ffn"),
        ),
        out_specs=(P("expert", None, "ffn"), P("expert", "ffn", None)),
        check_vma=False,
    )
```

profile of v0, /device:TPU:1, one launch (start us, length us, event | category | flops | bytes accessed | tf_op | source)
XLA Modules:
  0.0 544.9 jit_solution(16337537194217358825)
XLA Ops:
  0.6 0.8 fusion.24
  1.6 0.8 select_reduce_fusion
  2.5 0.7 multiply_add_fusion.5
  3.1 1.6 convolution_convert_fusion
  4.7 2.4 reshape.85
  7.1 1.9 copy.12
  9.0 19.1 %all-to-all-start.1 = ((bf16[20,64,512]{2,0,1:T(8,128)(2,1)}), bf16[20,64,512]{2,0,1:T(8,128)(2,1)S(1)}, u32[]{:S(2)}, u32[]{:S(2)}) async-start(bf16[20,64,512]{2,0,1:T(8,128)(2,1)} %copy.12), calls=%async_computation.1 | async-start | bytes 3145728 | tf_op jit(solution)/shard_map/all_to_all | solution.py:66
  28.1 2.8 convolution_convert_fusion.1
  30.9 3.3 reshape.83
  34.1 3.2 copy.11
  37.3 64.3 %all-to-all-done.1 = bf16[20,64,512]{2,0,1:T(8,128)(2,1)S(1)} async-done(((bf16[20,64,512]{2,0,1:T(8,128)(2,1)}), bf16[20,64,512]{2,0,1:T(8,128)(2,1)S(1)}, u32[]{:S(2)}, u32[]{:S(2)}) %all-to-all-start.1) | async-done | bytes 1310752 | tf_op jit(solution)/shard_map/all_to_all | solution.py:66
  101.6 9.8 %all-to-all-start = ((bf16[20,64,512]{2,0,1:T(8,128)(2,1)}), bf16[20,64,512]{2,0,1:T(8,128)(2,1)}, u32[]{:S(2)}, u32[]{:S(2)}) async-start(bf16[20,64,512]{2,0,1:T(8,128)(2,1)} %copy.11), calls=%async_computation | async-start | bytes 3145728 | tf_op jit(solution)/shard_map/all_to_all | solution.py:65
  111.4 1.2 reshape.86
  112.6 71.3 %all-to-all-done = bf16[20,64,512]{2,0,1:T(8,128)(2,1)} async-done(((bf16[20,64,512]{2,0,1:T(8,128)(2,1)}), bf16[20,64,512]{2,0,1:T(8,128)(2,1)}, u32[]{:S(2)}, u32[]{:S(2)}) %all-to-all-start) | async-done | bytes 1310752 | tf_op jit(solution)/shard_map/all_to_all | solution.py:65
  184.0 3.3 reshape.84
  187.3 1.2 convolution_bitcast_fusion
  188.7 1.2 convolution_bitcast_fusion.1
  190.4 2.2 broadcast_select_fusion
  192.6 0.5 copy-done.3
  193.2 4.8 collective-permute-start
  198.0 66.7 %collective-permute-done = f32[2,640,640]{2,1,0:T(8,128)} collective-permute-done((f32[2,640,640]{2,1,0:T(8,128)}, f32[2,640,640]{2,1,0:T(8,128)}, u32[]{:S(2)}, u32[]{:S(2)}) %collective-permute-start) | collective-permute-done | bytes 3276832 | tf_op jit(solution)/shard_map/ppermute | solution.py:22
  264.7 4.3 select_add_fusion
  269.2 1.5 copy-done.1
  270.7 6.2 %collective-permute-start.1 = (f32[2,320,640]{2,1,0:T(8,128)S(1)}, f32[2,320,640]{2,1,0:T(8,128)}, u32[]{:S(2)}, u32[]{:S(2)}) collective-permute-start(f32[2,320,640]{2,1,0:T(8,128)S(1)} %slice_select_fusion), channel_id=1, source_target_pairs={{0,16},{8,24},{16,0},{24,8},{32,48},{40,56},{48,32},{56,40},{64,80... | collective-permute-start | bytes 4915208 | tf_op jit(solution)/shard_map/ppermute | solution.py:22
  276.9 31.6 %collective-permute-done.1 = f32[2,320,640]{2,1,0:T(8,128)} collective-permute-done((f32[2,320,640]{2,1,0:T(8,128)S(1)}, f32[2,320,640]{2,1,0:T(8,128)}, u32[]{:S(2)}, u32[]{:S(2)}) %collective-permute-start.1) | collective-permute-done | bytes 1638432 | tf_op jit(solution)/shard_map/ppermute | solution.py:22
  308.5 2.6 select_add_fusion.1
  311.3 5.2 collective-permute-start.2
  316.4 14.3 %collective-permute-done.2 = f32[2,160,640]{2,1,0:T(8,128)S(1)} collective-permute-done((f32[2,160,640]{2,1,0:T(8,128)S(1)}, f32[2,160,640]{2,1,0:T(8,128)S(1)}, u32[]{:S(2)}, u32[]{:S(2)}) %collective-permute-start.2) | collective-permute-done | bytes 819232 | tf_op jit(solution)/shard_map/ppermute | solution.py:22
  330.9 3.1 collective-permute-start.3
  334.0 13.8 %collective-permute-done.3 = f32[2,160,640]{2,1,0:T(8,128)S(1)} collective-permute-done((f32[2,160,640]{2,1,0:T(8,128)S(1)}, f32[2,160,640]{2,1,0:T(8,128)S(1)}, u32[]{:S(2)}, u32[]{:S(2)}) %collective-permute-start.3) | collective-permute-done | bytes 819232 | tf_op jit(solution)/shard_map/ppermute | solution.py:22
  347.9 1.9 collective-permute-start.4
  349.8 33.1 %collective-permute-done.4 = f32[2,320,640]{2,1,0:T(8,128)S(1)} collective-permute-done((f32[2,320,640]{2,1,0:T(8,128)S(1)}, f32[2,320,640]{2,1,0:T(8,128)S(1)}, u32[]{:S(2)}, u32[]{:S(2)}) %collective-permute-start.4) | collective-permute-done | bytes 1638432 | tf_op jit(solution)/shard_map/ppermute | solution.py:22
  383.2 4.1 collective-permute-start.5
  387.2 62.3 %collective-permute-done.5 = f32[2,640,640]{2,1,0:T(8,128)S(1)} collective-permute-done((f32[2,640,640]{2,1,0:T(8,128)S(1)}, f32[2,640,640]{2,1,0:T(8,128)S(1)}, u32[]{:S(2)}, u32[]{:S(2)}) %collective-permute-start.5) | collective-permute-done | bytes 3276832 | tf_op jit(solution)/shard_map/ppermute | solution.py:22
  449.6 0.7 maximum_select_fusion
  450.3 2.6 fusion.17
  452.9 2.4 fusion.18
  455.3 3.1 collective-permute-start.6
  458.4 1.3 collective-permute-done.6
  459.7 8.4 %collective-permute-start.7 = (f32[2,640]{1,0:T(2,128)S(1)}, f32[2,640]{1,0:T(2,128)S(1)}, u32[]{:S(2)}, u32[]{:S(2)}) collective-permute-start(f32[2,640]{1,0:T(2,128)S(1)} %fusion.40), channel_id=1, source_target_pairs={{0,16},{8,24},{16,0},{24,8},{32,48},{40,56},{48,32},{56,40},{64,80... | collective-permute-start | bytes 15368 | tf_op jit(solution)/shard_map/ppermute | solution.py:22
  468.1 1.0 collective-permute-done.7
  469.1 2.5 collective-permute-start.8
  471.7 0.8 dynamic-slice_multiply_fusion.2
  472.5 1.5 dynamic-slice_reduce_fusion
  474.7 1.3 multiply_reduce_fusion.3
  476.0 1.4 fusion.29
  477.4 2.0 pad_maximum_fusion.2
  479.4 20.8 %all-reduce = (f32[3]{0:T(128)S(1)}, f32[512]{0:T(512)S(1)}, f32[512]{0:T(512)S(1)}) all-reduce(f32[3]{0:T(128)S(1)} %pad_maximum_fusion.2, f32[512]{0:T(512)S(1)} %get-tuple-element.4, f32[512]{0:T(512)S(1)} %get-tuple-element.2), channel_id=1, replica_groups=mesh['expert'=64,'ffn'=8] {'ffn'}, use_global_device_ids=true, to_apply=%region_10.11 | all-reduce | flops 1027 | bytes 8216 | tf_op jit(solution)/shard_map/psum | solution.py:115
  500.2 0.6 fusion.42
  502.9 1.2 multiply_reduce_fusion.1
  504.1 1.1 multiply_reduce_fusion
  505.2 1.3 pad_maximum_fusion.3
  506.6 3.1 collective-permute-start.9
  509.7 1.2 collective-permute-done.9
  510.9 1.3 fusion.49
  512.2 5.1 collective-permute-start.10
  517.4 0.9 collective-permute-done.10
  518.3 1.3 fusion.51
  519.7 2.5 collective-permute-start.11
  522.1 1.8 collective-permute-done.11
  524.0 15.4 %psum.31 = f32[2]{0:T(128)S(1)} all-reduce(f32[2]{0:T(128)S(1)} %add.143), channel_id=1, replica_groups=mesh['expert'=64,'ffn'=8] {'ffn'}, use_global_device_ids=true, to_apply=%region_15.16 | all-reduce | flops 2 | bytes 16 | tf_op jit(solution)/shard_map/psum | solution.py:128
  539.4 0.6 fusion.41
  540.6 2.5 fusion.23
  543.7 1.1 fusion.22
  (37 shorter events, 1.8 us)
Async XLA Ops:
  0.6 2.5 copy-start
  9.0 92.6 %all-to-all-start.1 = ((bf16[20,64,512]{2,0,1:T(8,128)(2,1)}), bf16[20,64,512]{2,0,1:T(8,128)(2,1)S(1)}, u32[]{:S(2)}, u32[]{:S(2)}) async-start(bf16[20,64,512]{2,0,1:T(8,128)(2,1)} %copy.12), calls=%async_computation.1 | async-start | bytes 3145728 | tf_op jit(solution)/shard_map/all_to_all | solution.py:66
  101.6 82.3 %all-to-all-start = ((bf16[20,64,512]{2,0,1:T(8,128)(2,1)}), bf16[20,64,512]{2,0,1:T(8,128)(2,1)}, u32[]{:S(2)}, u32[]{:S(2)}) async-start(bf16[20,64,512]{2,0,1:T(8,128)(2,1)} %copy.11), calls=%async_computation | async-start | bytes 3145728 | tf_op jit(solution)/shard_map/all_to_all | solution.py:65
  112.6 74.6 %copy-start.5 = (bf16[1280,512]{1,0:T(8,128)(2,1)S(1)}, bf16[1280,512]{1,0:T(8,128)(2,1)}, u32[]{:S(2)}) copy-start(bf16[1280,512]{1,0:T(8,128)(2,1)} %reshape.86) | copy-start | bytes 3932164
  112.6 74.6 %copy-start.9 = (bf16[1,640,512]{2,1,0:T(8,128)(2,1)S(1)}, bf16[1,640,512]{2,1,0:T(8,128)(2,1)}, u32[]{:S(2)}) copy-start(bf16[1,640,512]{2,1,0:T(8,128)(2,1)} %param.11) | copy-start | bytes 1966084
  187.2 1.3 copy-start.7
  187.2 1.5 copy-start.10
  188.7 1.7 copy-start.2
  190.4 2.8 copy-start.3
  193.2 71.6 %collective-permute-start = (f32[2,640,640]{2,1,0:T(8,128)}, f32[2,640,640]{2,1,0:T(8,128)}, u32[]{:S(2)}, u32[]{:S(2)}) collective-permute-start(f32[2,640,640]{2,1,0:T(8,128)} %broadcast_select_fusion), channel_id=1, source_target_pairs={{0,8},{8,0},{16,24},{24,16},{32,40},{40,32},{48,56},{56,48},{64,72... | collective-permute-start | bytes 9830408 | tf_op jit(solution)/shard_map/ppermute | solution.py:22
  269.0 1.7 copy-start.1
  270.7 37.9 %collective-permute-start.1 = (f32[2,320,640]{2,1,0:T(8,128)S(1)}, f32[2,320,640]{2,1,0:T(8,128)}, u32[]{:S(2)}, u32[]{:S(2)}) collective-permute-start(f32[2,320,640]{2,1,0:T(8,128)S(1)} %slice_select_fusion), channel_id=1, source_target_pairs={{0,16},{8,24},{16,0},{24,8},{32,48},{40,56},{48,32},{56,40},{64,80... | collective-permute-start | bytes 4915208 | tf_op jit(solution)/shard_map/ppermute | solution.py:22
  311.3 19.5 %collective-permute-start.2 = (f32[2,160,640]{2,1,0:T(8,128)S(1)}, f32[2,160,640]{2,1,0:T(8,128)S(1)}, u32[]{:S(2)}, u32[]{:S(2)}) collective-permute-start(f32[2,160,640]{2,1,0:T(8,128)S(1)} %slice_select_fusion.1), channel_id=1, source_target_pairs={{0,32},{8,40},{16,48},{24,56},{32,0},{40,8},{48,16},{56,24},{64,96... | collective-permute-start | bytes 2457608 | tf_op jit(solution)/shard_map/ppermute | solution.py:22
  330.9 16.9 %collective-permute-start.3 = (f32[2,160,640]{2,1,0:T(8,128)S(1)}, f32[2,160,640]{2,1,0:T(8,128)S(1)}, u32[]{:S(2)}, u32[]{:S(2)}) collective-permute-start(f32[2,160,640]{2,1,0:T(8,128)S(1)} %select_add_fusion.2), channel_id=1, source_target_pairs={{0,32},{8,40},{16,48},{24,56},{32,0},{40,8},{48,16},{56,24},{64,96... | collective-permute-start | bytes 2457608 | tf_op jit(solution)/shard_map/ppermute | solution.py:22
  347.9 35.1 %collective-permute-start.4 = (f32[2,320,640]{2,1,0:T(8,128)S(1)}, f32[2,320,640]{2,1,0:T(8,128)S(1)}, u32[]{:S(2)}, u32[]{:S(2)}) collective-permute-start(f32[2,320,640]{2,1,0:T(8,128)S(1)} %maximum_select_fusion.2), channel_id=1, source_target_pairs={{0,16},{8,24},{16,0},{24,8},{32,48},{40,56},{48,32},{56,40},{64,80... | collective-permute-start | bytes 4915208 | tf_op jit(solution)/shard_map/ppermute | solution.py:22
  383.2 67.1 %copy-start.8 = (bf16[1280,512]{1,0:T(8,128)(2,1)S(1)}, bf16[1280,512]{1,0:T(8,128)(2,1)}, u32[]{:S(2)}) copy-start(bf16[1280,512]{1,0:T(8,128)(2,1)} %reshape.84) | copy-start | bytes 3932164
  383.2 66.4 %collective-permute-start.5 = (f32[2,640,640]{2,1,0:T(8,128)S(1)}, f32[2,640,640]{2,1,0:T(8,128)S(1)}, u32[]{:S(2)}, u32[]{:S(2)}) collective-permute-start(f32[2,640,640]{2,1,0:T(8,128)S(1)} %maximum_select_fusion.1), channel_id=1, source_target_pairs={{0,8},{8,0},{16,24},{24,16},{32,40},{40,32},{48,56},{56,48},{64,72... | collective-permute-start | bytes 9830408 | tf_op jit(solution)/shard_map/ppermute | solution.py:22
  450.3 2.6 copy-start.6
  455.3 4.4 collective-permute-start.6
  459.7 9.4 %collective-permute-start.7 = (f32[2,640]{1,0:T(2,128)S(1)}, f32[2,640]{1,0:T(2,128)S(1)}, u32[]{:S(2)}, u32[]{:S(2)}) collective-permute-start(f32[2,640]{1,0:T(2,128)S(1)} %fusion.40), channel_id=1, source_target_pairs={{0,16},{8,24},{16,0},{24,8},{32,48},{40,56},{48,32},{56,40},{64,80... | collective-permute-start | bytes 15368 | tf_op jit(solution)/shard_map/ppermute | solution.py:22
  469.1 6.9 %collective-permute-start.8 = (f32[2,640]{1,0:T(2,128)S(1)}, f32[2,640]{1,0:T(2,128)S(1)}, u32[]{:S(2)}, u32[]{:S(2)}) collective-permute-start(f32[2,640]{1,0:T(2,128)S(1)} %fusion.50), channel_id=1, source_target_pairs={{0,32},{8,40},{16,48},{24,56},{32,0},{40,8},{48,16},{56,24},{64,96... | collective-permute-start | bytes 15368 | tf_op jit(solution)/shard_map/ppermute | solution.py:22
  502.1 2.0 copy-start.4
  506.6 4.3 collective-permute-start.9
  512.2 6.1 %collective-permute-start.10 = (f32[2]{0:T(128)S(1)}, f32[2]{0:T(128)S(1)}, u32[]{:S(2)}, u32[]{:S(2)}) collective-permute-start(f32[2]{0:T(128)S(1)} %fusion.49), channel_id=1, source_target_pairs={{0,16},{8,24},{16,0},{24,8},{32,48},{40,56},{48,32},{56,40},{64,80... | collective-permute-start | bytes 32 | tf_op jit(solution)/shard_map/ppermute | solution.py:22
  519.7 4.3 collective-permute-start.11
where the time goes:
time: 553 us; the launch traced here: 545 us
  waiting for transfers between devices  364 us (66%)
  starting transfers between devices  78.9 us (14%)
  blocking collectives  36.2 us (7%)
  other arithmetic  30.2 us (5%)
  local copies, waits for them, and re-layouts  19.2 us (3%)
  matrix products  11.7 us (2%)
    ppermute x12, waiting for transfers between devices, partner_2(): return lax.ppermute(value, axis, pairs)  228 us
    all_to_all x1, waiting for transfers between devices, shards(): lax.all_to_all(sent_tokens, 'expert', split_axis=1, concat_axis=0, tiled=...  71.3 us
    all_to_all x1, waiting for transfers between devices, shards(): lax.all_to_all(sent_cotangent, 'expert', split_axis=1, concat_axis=0, til...  64.3 us
    ppermute x12, starting transfers between devices, partner_2(): return lax.ppermute(value, axis, pairs)  50 us
    psum x1, blocking collectives, shards(): lax.psum((jnp.sum(square_in, axis=1), jnp.sum(square_out, axis=0), small_...  20.8 us
    all_to_all x1, starting transfers between devices, shards(): lax.all_to_all(sent_cotangent, 'expert', split_axis=1, concat_axis=0, til...  19.1 us
    psum x1, blocking collectives, shards(): norm_sums = lax.psum(norm_sums, 'ffn')  15.4 us
  transfers between devices with their start and end apart: 14, of which 13 were waited for; matrix products, arithmetic and copies ran while one was open for 3% of the time, Pallas kernels for 0%

commit v1 on v0

v1 whole, which is shorter than its diff:
```python
import math

import jax
import jax.numpy as jnp
from jax import lax
from jax.experimental import pallas as pl
from jax.experimental.pallas import tpu as pltpu
from jax.sharding import PartitionSpec as P

D = 4096
FF = 5120
GROUP = 8
EXPERTS = 8
FFN = 8
CAP = 20
BLK = D // GROUP
HID = FF // FFN
TOK = 128
ROWS = GROUP * CAP
PIECES = 8

DECAY_RATE = 0.9
EPS_ONE = 1e-30
ROOT_COEF = math.sqrt(2.0 / math.pi)
CUBIC_COEF = 0.044715

MESH = pl.DeviceIdType.MESH
F32 = jnp.float32
BF16 = jnp.bfloat16
NT = (((1,), (1,)), ((), ()))
TN = (((0,), (0,)), ((), ()))


def gelu_pair(inputs):
    inner = ROOT_COEF * (inputs + CUBIC_COEF * inputs * inputs * inputs)
    tangent = jnp.tanh(inner)
    act_value = 0.5 * inputs * (1.0 + tangent)
    act_slope = 0.5 * (1.0 + tangent) + 0.5 * inputs * (1.0 - tangent * tangent) * ROOT_COEF * (
        1.0 + 3.0 * CUBIC_COEF * inputs * inputs
    )
    return (act_value, act_slope)


def iota(shape, dim):
    return lax.broadcasted_iota(jnp.int32, shape, dim)


def kernel(
    ids_ref, tok_ref, cot_ref, win_ref, wout_ref, ws_ref, hs_ref,
    uin_ref, uout_ref,
    chunk_s, chunk_r, xall, part_s, part_r, acc, hp, gin, gout,
    lane_in, lane_out, stat_h, stat_w, norm_g, norm_f,
    a2a_ss, a2a_rs, ring_ss, ring_rs, rs_ss, rs_rs, ag_ss, ag_rs,
    sh_ss, sh_rs, sw_ss, sw_rs, ng_ss, ng_rs, nf_ss, nf_rs,
):
    p = lax.axis_index("expert")
    f = lax.axis_index("ffn")
    e = p // GROUP
    i = p % GROUP
    y = f // 2
    core = f % 2

    def turn(value, n):
        return lax.rem(value, n)

    def chunk_of(ff):
        return turn(ff + 2 * GROUP - i - e, GROUP)

    mine = chunk_of(f)
    f_pair = y * 2 + (1 - core)
    f_up = turn(y + 1, 4) * 2 + core
    f_dn = turn(y + 3, 4) * 2 + core
    f_op = turn(y + 2, 4) * 2 + core

    def pair_of(ff):
        return (ff // 2) * 2 + (1 - ff % 2)

    barrier = pltpu.get_barrier_semaphore()
    for q in range(EXPERTS):
        source = q * GROUP + mine

        @pl.when(source != p)
        def _():
            pl.semaphore_signal(barrier, inc=1, device_id=(source, f), device_id_type=MESH)

    for k in range(1, GROUP):
        pl.semaphore_signal(
            barrier, inc=1, device_id=(e * GROUP + turn(i + k, GROUP), f), device_id_type=MESH
        )
        pl.semaphore_signal(barrier, inc=1, device_id=(p, turn(f + k, FFN)), device_id_type=MESH)

    ids = ids_ref[...]
    onehot = iota((EXPERTS, TOK), 0) == ids
    earlier = jnp.where(iota((TOK, TOK), 0) < iota((TOK, TOK), 1), 1.0, 0.0).astype(BF16)
    before = jnp.dot(
        jnp.where(onehot, 1.0, 0.0).astype(BF16), earlier, preferred_element_type=F32
    )
    slot = jnp.sum(jnp.where(onehot, before, 0.0), axis=0, keepdims=True).astype(jnp.int32)
    pieces_row = iota((ROWS, PIECES * TOK), 0) - CAP * (iota((ROWS, PIECES * TOK), 1) // TOK)

    def build(expert, carry):
        place = jnp.where(ids == expert, slot, -ROWS * 2)
        place = jnp.concatenate([place] * PIECES, axis=1)
        select = jnp.where(pieces_row == place, 1.0, 0.0).astype(BF16)
        offset = turn(f + 2 * GROUP - expert - i, GROUP) * BLK
        parts = []
        for ref in (tok_ref, cot_ref):
            for g in range(4):
                parts.append(ref[:, pl.ds(pl.multiple_of(offset + g * 128, 128), 128)])
        chunk_s[expert] = jnp.dot(
            select, jnp.concatenate(parts, axis=0), preferred_element_type=F32
        ).astype(BF16)
        return carry

    lax.fori_loop(0, EXPERTS, build, 0)

    pl.semaphore_wait(barrier, EXPERTS + 2 * (GROUP - 1) - jnp.where(mine == i, 1, 0))

    def routed(expert):
        target = expert * GROUP + turn(f + 2 * GROUP - expert - i, GROUP)
        copy = pltpu.make_async_remote_copy(
            src_ref=chunk_s.at[expert], dst_ref=chunk_r.at[e],
            send_sem=a2a_ss.at[expert], recv_sem=a2a_rs.at[e],
            device_id=(target, f), device_id_type=MESH,
        )
        return target, copy

    for k in range(EXPERTS):
        target, copy = routed(turn(e + 4 + k, EXPERTS))

        @pl.when(target != p)
        def _():
            copy.start()

        @pl.when(target == p)
        def _():
            chunk_r[e] = chunk_s[e]

    def landed(q):
        return pltpu.make_async_remote_copy(
            src_ref=chunk_s.at[q], dst_ref=chunk_r.at[q],
            send_sem=a2a_ss.at[q], recv_sem=a2a_rs.at[q],
            device_id=(p, f), device_id_type=MESH,
        )

    for q in range(EXPERTS):
        @pl.when(q * GROUP + mine != p)
        def _():
            landed(q).wait_recv()

    received = chunk_r[...].reshape(EXPERTS * ROWS, 128)
    row_of = iota((ROWS, EXPERTS * ROWS), 0)
    source_of = lax.shift_right_logical(row_of * 3277, 16)
    gap = iota((ROWS, EXPERTS * ROWS), 1) - (ROWS - CAP) * source_of - row_of
    for piece in range(PIECES):
        select = jnp.where(gap == CAP * piece, 1.0, 0.0).astype(BF16)
        xall[mine, :, piece * 128 : (piece + 1) * 128] = jnp.dot(
            select, received, preferred_element_type=F32
        ).astype(BF16)

    def ring(c, start, size, target, index):
        rows = pl.ds(start, size)
        return pltpu.make_async_remote_copy(
            src_ref=xall.at[c, rows], dst_ref=xall.at[c, rows],
            send_sem=ring_ss.at[index], recv_sem=ring_rs.at[index],
            device_id=(p, target), device_id_type=MESH,
        )

    half = ROWS // 2
    c_pair, c_up, c_dn, c_op = chunk_of(f_pair), chunk_of(f_up), chunk_of(f_dn), chunk_of(f_op)
    to_up = ring(mine, 0, ROWS, f_up, 0)
    to_dn = ring(mine, 0, ROWS, f_dn, 1)
    to_pair = ring(mine, 0, ROWS, f_pair, 2)
    on_up = ring(c_dn, 0, half, f_up, 3)
    on_dn = ring(c_up, half, half, f_dn, 4)
    pair_dn = ring(c_dn, 0, ROWS, f_pair, 5)
    pair_up = ring(c_up, 0, ROWS, f_pair, 6)
    pair_op_a = ring(c_op, 0, half, f_pair, 7)
    pair_op_b = ring(c_op, half, half, f_pair, 8)
    sent = [to_up, to_dn, to_pair, on_up, on_dn, pair_dn, pair_up, pair_op_a, pair_op_b]

    def partial_copy(c):
        return pltpu.make_async_remote_copy(
            src_ref=part_s.at[c], dst_ref=part_r.at[i],
            send_sem=rs_ss.at[c], recv_sem=rs_rs.at[i],
            device_id=(e * GROUP + c, f), device_id_type=MESH,
        )

    def partial_landed(d):
        return pltpu.make_async_remote_copy(
            src_ref=part_s.at[d], dst_ref=part_r.at[d],
            send_sem=rs_ss.at[d], recv_sem=rs_rs.at[d],
            device_id=(e * GROUP + d, f), device_id_type=MESH,
        )

    def partials(c):
        pre = jnp.dot(xall[c, :, :BLK], win_ref[...], preferred_element_type=F32)
        back = lax.dot_general(xall[c, :, BLK:], wout_ref[...], NT, preferred_element_type=F32)

        @pl.when(c == i)
        def _():
            acc[:, :HID] = pre
            acc[:, HID:] = back

        @pl.when(c != i)
        def _():
            part_s[c, :, :HID] = pre.astype(BF16)
            part_s[c, :, HID:] = back.astype(BF16)
            partial_copy(c).start()

    to_up.start()
    to_dn.start()
    to_pair.start()
    partials(mine)
    ring(c_pair, 0, ROWS, f_pair, 2).wait_recv()
    partials(c_pair)
    ring(c_dn, 0, ROWS, f_dn, 0).wait_recv()
    on_up.start()
    pair_dn.start()
    ring(c_up, 0, ROWS, f_up, 1).wait_recv()
    on_dn.start()
    pair_up.start()
    partials(c_dn)
    partials(c_up)
    ring(chunk_of(pair_of(f_dn)), 0, ROWS, f_pair, 5).wait_recv()
    partials(chunk_of(pair_of(f_dn)))
    ring(c_op, 0, half, f_dn, 3).wait_recv()
    pair_op_a.start()
    ring(c_op, half, half, f_up, 4).wait_recv()
    pair_op_b.start()
    ring(chunk_of(pair_of(f_up)), 0, ROWS, f_pair, 6).wait_recv()
    partials(chunk_of(pair_of(f_up)))
    partials(c_op)
    c_last = chunk_of(pair_of(f_op))
    ring(c_last, 0, half, f_pair, 7).wait_recv()
    ring(c_last, half, half, f_pair, 8).wait_recv()
    partials(c_last)

    for k in range(1, GROUP):
        d = turn(i + k, GROUP)
        partial_landed(d).wait_recv()
        acc[...] += part_r[d].astype(F32)

    def activate(block, carry):
        rows = pl.ds(pl.multiple_of(block * 16, 16), 16)
        act_value, act_slope = gelu_pair(acc[rows, :HID])
        hp[i, rows, :HID] = act_value.astype(BF16)
        hp[i, rows, HID:] = (acc[rows, HID:] * act_slope).astype(BF16)
        return carry

    lax.fori_loop(0, ROWS // 16, activate, 0)

    def finished(c, target):
        return pltpu.make_async_remote_copy(
            src_ref=hp.at[c], dst_ref=hp.at[c],
            send_sem=ag_ss.at[target], recv_sem=ag_rs.at[c],
            device_id=(e * GROUP + target, f), device_id_type=MESH,
        )

    for k in range(1, GROUP):
        finished(i, turn(i + k, GROUP)).start()

    for k in range(GROUP):
        d = turn(i + k, GROUP)
        if k:
            finished(d, d).wait_recv()
        add_in = lax.dot_general(
            xall[d, :, :BLK], hp[d, :, HID:], TN, preferred_element_type=F32
        )
        add_out = lax.dot_general(
            hp[d, :, :HID], xall[d, :, BLK:], TN, preferred_element_type=F32
        )
        if k:
            gin[...] += add_in
            gout[...] += add_out
        else:
            gin[...] = add_in
            gout[...] = add_out

    def squares(ref, lanes, width, rows):
        def step(block, total):
            here = pl.ds(pl.multiple_of(block * 32, 32), 32)
            value = ref[here, :]
            value = value * value + EPS_ONE
            folded = value[:, :128]
            for g in range(1, width // 128):
                folded = folded + value[:, g * 128 : (g + 1) * 128]
            lanes[here, :] = folded
            return total + jnp.sum(value.reshape(4, 8, width), axis=0)

        total = lax.fori_loop(0, rows // 32, step, jnp.zeros((8, width), F32))
        return jnp.sum(total, axis=0, keepdims=True), jnp.sum(lanes[...].T, axis=0, keepdims=True)

    cols_in, rows_in = squares(gin, lane_in, HID, BLK)
    cols_out, rows_out = squares(gout, lane_out, BLK, HID)
    hidden_prev = hs_ref[:, pl.ds(e, 1), :]
    width_prev = ws_ref[:, pl.ds(e, 1), pl.ds(pl.multiple_of(i * BLK, BLK), BLK)]
    hidden_sum = jnp.sum(hidden_prev[1], axis=1, keepdims=True)
    stat_h[i] = jnp.concatenate([cols_in, rows_out, jnp.zeros((6, HID), F32)], axis=0)
    stat_w[f] = jnp.concatenate(
        [rows_in, cols_out, jnp.broadcast_to(hidden_sum, (6, BLK))], axis=0
    )

    def exchange(buf, own, ssem, rsem, device):
        copies = []
        for k in range(1, 8):
            d = turn(own + k, 8)
            copies.append((
                pltpu.make_async_remote_copy(
                    src_ref=buf.at[own], dst_ref=buf.at[own],
                    send_sem=ssem.at[d], recv_sem=rsem.at[own],
                    device_id=device(d), device_id_type=MESH,
                ),
                pltpu.make_async_remote_copy(
                    src_ref=buf.at[d], dst_ref=buf.at[d],
                    send_sem=ssem.at[d], recv_sem=rsem.at[d],
                    device_id=device(d), device_id_type=MESH,
                ),
            ))
        return copies

    def in_group(d):
        return (e * GROUP + d, f)

    def in_ffn(d):
        return (p, d)

    over_group = exchange(stat_h, i, sh_ss, sh_rs, in_group)
    over_ffn = exchange(stat_w, f, sw_ss, sw_rs, in_ffn)
    for start, _ in over_group + over_ffn:
        start.start()
    for _, arrival in over_group + over_ffn:
        arrival.wait_recv()
    sum_h = jnp.sum(stat_h[...], axis=0)
    sum_w = jnp.sum(stat_w[...], axis=0)

    cols_in = DECAY_RATE * hidden_prev[0] + (1.0 - DECAY_RATE) * sum_h[0:1] / D
    rows_out = DECAY_RATE * hidden_prev[1] + (1.0 - DECAY_RATE) * sum_h[1:2] / D
    rows_in = DECAY_RATE * width_prev[0] + (1.0 - DECAY_RATE) * sum_w[0:1] / FF
    cols_out = DECAY_RATE * width_prev[1] + (1.0 - DECAY_RATE) * sum_w[1:2] / FF
    lane_in[...] = jnp.broadcast_to(lax.rsqrt(rows_in), (128, BLK)).T
    lane_out[...] = jnp.broadcast_to(lax.rsqrt(rows_out), (128, HID)).T
    scale_in = lax.rsqrt(cols_in)
    scale_out = lax.rsqrt(cols_out)

    def scaled(ref, lanes, scale, width, rows):
        def step(block, total):
            here = pl.ds(pl.multiple_of(block * 32, 32), 32)
            factor = lanes[here, :]
            for g in range(width // 128):
                cols = slice(g * 128, (g + 1) * 128)
                value = ref[here, cols] * factor * scale[:, cols]
                ref[here, cols] = value
                total = total + jnp.sum((value * value).reshape(4, 8, 128), axis=0)
            return total

        total = lax.fori_loop(0, rows // 32, step, jnp.zeros((8, 128), F32))
        return jnp.sum(total, axis=0, keepdims=True)

    norm_in = scaled(gin, lane_in, scale_in, HID, BLK)
    norm_out = scaled(gout, lane_out, scale_out, BLK, HID)

    def fold(row):
        total = row[:, :128]
        for g in range(1, row.shape[1] // 128):
            total = total + row[:, g * 128 : (g + 1) * 128]
        return total

    norm_g[i] = jnp.concatenate(
        [norm_in, norm_out, fold(sum_w[0:1]), fold(sum_w[1:2]), jnp.zeros((4, 128), F32)], axis=0
    )
    group_norms = exchange(norm_g, i, ng_ss, ng_rs, in_group)
    for start, _ in group_norms:
        start.start()
    for _, arrival in group_norms:
        arrival.wait_recv()
    group_sum = jnp.sum(norm_g[...], axis=0)
    norm_f[f] = group_sum
    ffn_norms = exchange(norm_f, f, nf_ss, nf_rs, in_ffn)
    for start, _ in ffn_norms:
        start.start()
    for _, arrival in ffn_norms:
        arrival.wait_recv()
    norm_sum = jnp.sum(jnp.sum(norm_f[...], axis=0), axis=1, keepdims=True)
    totals = jnp.sum(group_sum, axis=1, keepdims=True)

    whole_count = float(D) * float(FF)
    width_mean = jnp.sum(ws_ref[0, pl.ds(e, 1), :], axis=1, keepdims=True) / D
    mean_in = DECAY_RATE * width_mean + (1.0 - DECAY_RATE) * totals[2:3] / whole_count
    mean_out = (
        DECAY_RATE * sum_w[2:3, 0:1] / FF + (1.0 - DECAY_RATE) * totals[3:4] / whole_count
    )
    def last_factor(mean, norm):
        return jnp.sqrt(mean) / jnp.maximum(1.0, jnp.sqrt(mean * (norm / whole_count)))

    factor_in = last_factor(mean_in, norm_sum[0:1])
    factor_out = last_factor(mean_out, norm_sum[1:2])

    def store_in(block, carry):
        here = pl.ds(pl.multiple_of(block * 32, 32), 32)
        uin_ref[here, :] = (gin[here, :] * factor_in).astype(BF16)
        return carry

    def store_out(block, carry):
        here = pl.ds(pl.multiple_of(block * 32, 32), 32)
        uout_ref[here, :] = (gout[here, :] * factor_out).astype(BF16)
        return carry

    lax.fori_loop(0, BLK // 32, store_in, 0)
    lax.fori_loop(0, HID // 32, store_out, 0)

    for q in range(EXPERTS):
        target, copy = routed(q)

        @pl.when(target != p)
        def _():
            copy.wait_send()

    for copy in sent:
        copy.wait_send()
    for k in range(1, GROUP):
        partial_copy(turn(i + k, GROUP)).wait_send()
        finished(i, turn(i + k, GROUP)).wait_send()
    for start, _ in over_group + over_ffn + group_norms + ffn_norms:
        start.wait_send()


def shards(tokens, cotangent, expert_ids, in_weight, out_weight, width_states, hidden_states):
    vmem = pl.BlockSpec(memory_space=pltpu.VMEM)
    dma8 = pltpu.SemaphoreType.DMA((8,))
    update_in, update_out = pl.pallas_call(
        kernel,
        out_shape=(
            jax.ShapeDtypeStruct((BLK, HID), BF16),
            jax.ShapeDtypeStruct((HID, BLK), BF16),
        ),
        in_specs=[vmem] * 7,
        out_specs=(vmem, vmem),
        scratch_shapes=[
            pltpu.VMEM((EXPERTS, ROWS, 128), BF16),
            pltpu.VMEM((EXPERTS, ROWS, 128), BF16),
            pltpu.VMEM((GROUP, ROWS, 2 * BLK), BF16),
            pltpu.VMEM((GROUP, ROWS, 2 * HID), BF16),
            pltpu.VMEM((GROUP, ROWS, 2 * HID), BF16),
            pltpu.VMEM((ROWS, 2 * HID), F32),
            pltpu.VMEM((GROUP, ROWS, 2 * HID), BF16),
            pltpu.VMEM((BLK, HID), F32),
            pltpu.VMEM((HID, BLK), F32),
            pltpu.VMEM((BLK, 128), F32),
            pltpu.VMEM((HID, 128), F32),
            pltpu.VMEM((GROUP, 8, HID), F32),
            pltpu.VMEM((FFN, 8, BLK), F32),
            pltpu.VMEM((GROUP, 8, 128), F32),
            pltpu.VMEM((FFN, 8, 128), F32),
            dma8, dma8,
            pltpu.SemaphoreType.DMA((9,)), pltpu.SemaphoreType.DMA((9,)),
            dma8, dma8, dma8, dma8, dma8, dma8, dma8, dma8, dma8, dma8, dma8, dma8,
        ],
        compiler_params=pltpu.CompilerParams(
            collective_id=0, has_side_effects=True, vmem_limit_bytes=56 * 1024 * 1024
        ),
        name="switch_update",
    )(
        expert_ids.reshape(1, TOK), tokens, cotangent, in_weight[0], out_weight[0],
        width_states, hidden_states,
    )
    return (update_in[None], update_out[None])


def solution(mesh):
    return jax.shard_map(
        shards,
        mesh=mesh,
        in_specs=(
            P("expert", None),
            P("expert", None),
            P("expert", None),
            P("expert", None, "ffn"),
            P("expert", "ffn", None),
            P(),
            P(None, None, "ffn"),
        ),
        out_specs=(P("expert", None, "ffn"), P("expert", "ffn", None)),
        check_vma=False,
    )
```

time: 553 us -> 168 us (0.30); the launches traced: 545 us -> 168 us
  waiting for transfers between devices: 364 us -> 0 us
  Pallas kernels: 0 us -> 165 us
  starting transfers between devices: 78.9 us -> 0 us
  blocking collectives: 36.2 us -> 0 us
  other arithmetic: 30.2 us -> 0 us
  local copies, waits for them, and re-layouts: 19.2 us -> 2.89 us
  matrix products: 11.7 us -> 0 us
    ppermute x12 -> x0, waiting for transfers between devices: 228 us -> none  [partner_2(): return lax.ppermute(value, axis, pairs)]
    pallas_call x0 -> x1, Pallas kernels: none -> 165 us  [shards(): pl.pallas_call(kernel, out_shape=(jax.ShapeDtypeStruct((BLK, HID), BF16),...]
    all_to_all x2 -> x0, waiting for transfers between devices: 136 us -> none  [the longest x1 71.3 us: shards(): lax.all_to_all(sent_tokens, 'expert', split_axis=1, concat_axis=0, tiled=...]
    ppermute x12 -> x0, starting transfers between devices: 50 us -> none  [partner_2(): return lax.ppermute(value, axis, pairs)]
    psum x2 -> x0, blocking collectives: 36.2 us -> none  [the longest x1 20.8 us: shards(): lax.psum((jnp.sum(square_in, axis=1), jnp.sum(square_out, axis=0), small_...]
    all_to_all x2 -> x0, starting transfers between devices: 28.9 us -> none  [the longest x1 19.1 us: shards(): lax.all_to_all(sent_cotangent, 'expert', split_axis=1, concat_axis=0, til...]
    reshape x6 -> x0, local copies, waits for them, and re-layouts: 15.2 us -> none  [the longest x2 6.44 us: shards(): sent_tokens = jnp.dot(select, tokens, preferred_element_type=jnp.float32)...]
    add x13 -> x0, other arithmetic: 11.8 us -> none  [the longest x3 7.05 us: shards(): partials = kept_rows + partner_2(sent_rows, 'expert', section)]
  transfers between devices with their start and end apart: 14 -> 0, of which waited for: 13 -> 0; matrix products, arithmetic and copies ran while one was open for 3% -> 0% of each run, Pallas kernels for 0% -> 0%
where the time goes in v1:
time: 168 us
  Pallas kernels  165 us (98%)
  local copies, waits for them, and re-layouts  2.89 us (2%)
    pallas_call x1, Pallas kernels, shards(): pl.pallas_call(kernel, out_shape=(jax.ShapeDtypeStruct((BLK, HID), BF16),...  165 us

profile of v1, /device:TPU:1, one launch (start us, length us, event | category | flops | bytes accessed | tf_op | source)
XLA Modules:
  0.0 168.1 jit_solution(555391137820554851)
XLA Ops:
  0.6 164.6 %switch_update.1 = (bf16[512,640]{1,0:T(8,128)(2,1)}, bf16[640,512]{1,0:T(8,128)(2,1)}) custom-call(s32[1,128]{1,0:T(1,128)} %bitcast.9, bf16[128,4096]{1,0:T(8,128)(2,1)} %tok_ref.1, bf16[128,4096]{1,0:T(8,128)(2,1)} %cot_ref.1, bf16[512,640]{1,0:T(8,128)(2,1)} %bitcast.7, bf16[640,512]{1,0:T(8,128)(2,1)} %bitcast.8, f32[2,8,4096]{2,1,0:T(8,128)} %ws_ref.1, ...), custom_call_target="tpu_custom_call" | custom-call | tf_op jit(solution)/shard_map/switch_update/pallas_call | solution.py:431
  165.2 0.0 copy-start
  165.2 2.0 %copy.11 = bf16[1,512,640]{2,1,0:T(8,128)(2,1)} copy(bf16[1,512,640]{2,1,0:T(8,128)(2,1)} %bitcast.6) | data formatting | bytes 1310720
  167.3 0.0 copy-done
  167.3 0.8 copy.12
Async XLA Ops:
  165.2 2.1 %copy-start = (bf16[640,512]{1,0:T(8,128)(2,1)S(1)}, bf16[640,512]{1,0:T(8,128)(2,1)}, u32[]{:S(2)}) copy-start(bf16[640,512]{1,0:T(8,128)(2,1)} %get-tuple-element.5) | copy-start | bytes 1966084

commit v2 on v1

--- a/solution.py
+++ b/solution.py
@@ -48,9 +48,9 @@
 def kernel(
     ids_ref, tok_ref, cot_ref, win_ref, wout_ref, ws_ref, hs_ref,
     uin_ref, uout_ref,
-    chunk_s, chunk_r, xall, part_s, part_r, acc, hp, gin, gout,
+    chunk_s, chunk_r, xall, part_s, relay_r, next_r, pair_r, work, acc, hp, gin, gout,
     lane_in, lane_out, stat_h, stat_w, norm_g, norm_f,
-    a2a_ss, a2a_rs, ring_ss, ring_rs, rs_ss, rs_rs, ag_ss, ag_rs,
+    a2a_ss, a2a_rs, ring_ss, ring_rs, rel_ss, rel_rs, nex_ss, nex_rs, par_ss, par_rs, ag_ss, ag_rs,
     sh_ss, sh_rs, sw_ss, sw_rs, ng_ss, ng_rs, nf_ss, nf_rs,
 ):
     p = lax.axis_index("expert")
@@ -63,17 +63,32 @@
     def turn(value, n):
         return lax.rem(value, n)
 
-    def chunk_of(ff):
-        return turn(ff + 2 * GROUP - i - e, GROUP)
-
-    mine = chunk_of(f)
-    f_pair = y * 2 + (1 - core)
-    f_up = turn(y + 1, 4) * 2 + core
-    f_dn = turn(y + 3, 4) * 2 + core
-    f_op = turn(y + 2, 4) * 2 + core
-
-    def pair_of(ff):
-        return (ff // 2) * 2 + (1 - ff % 2)
+    def flip(value, mask):
+        for bit in (1, 2, 4):
+            if mask & bit:
+                value = value + bit * (1 - 2 * turn(value // bit, 2))
+        return value
+
+    def xor(*values):
+        total = 0
+        for bit in (1, 2, 4):
+            total = total + bit * turn(sum(value // bit for value in values), 2)
+        return total
+
+    turned = core * 4 + y
+    mine = xor(turned, i, e)
+
+    def label(m):
+        return flip(mine, m ^ 6)
+
+    def over(d):
+        return flip(mine, (d % 2) * 4 + d // 2)
+
+    def place(m):
+        return (e * GROUP + flip(i, m), f)
+
+    def side(d):
+        return (p, flip(f, d))
 
     barrier = pltpu.get_barrier_semaphore()
     for q in range(EXPERTS):
@@ -102,7 +117,7 @@
         place = jnp.where(ids == expert, slot, -ROWS * 2)
         place = jnp.concatenate([place] * PIECES, axis=1)
         select = jnp.where(pieces_row == place, 1.0, 0.0).astype(BF16)
-        offset = turn(f + 2 * GROUP - expert - i, GROUP) * BLK
+        offset = xor(turned, expert, i) * BLK
         parts = []
         for ref in (tok_ref, cot_ref):
             for g in range(4):
@@ -117,7 +132,7 @@
     pl.semaphore_wait(barrier, EXPERTS + 2 * (GROUP - 1) - jnp.where(mine == i, 1, 0))
 
     def routed(expert):
-        target = expert * GROUP + turn(f + 2 * GROUP - expert - i, GROUP)
+        target = expert * GROUP + xor(turned, expert, i)
         copy = pltpu.make_async_remote_copy(
             src_ref=chunk_s.at[expert], dst_ref=chunk_r.at[e],
             send_sem=a2a_ss.at[expert], recv_sem=a2a_rs.at[e],
@@ -158,124 +173,166 @@
             select, received, preferred_element_type=F32
         ).astype(BF16)
 
-    def ring(c, start, size, target, index):
+    def ring(chunk, start, size, device, index):
         rows = pl.ds(start, size)
         return pltpu.make_async_remote_copy(
-            src_ref=xall.at[c, rows], dst_ref=xall.at[c, rows],
+            src_ref=xall.at[chunk, rows], dst_ref=xall.at[chunk, rows],
             send_sem=ring_ss.at[index], recv_sem=ring_rs.at[index],
-            device_id=(p, target), device_id_type=MESH,
+            device_id=device, device_id_type=MESH,
         )
 
     half = ROWS // 2
-    c_pair, c_up, c_dn, c_op = chunk_of(f_pair), chunk_of(f_up), chunk_of(f_dn), chunk_of(f_op)
-    to_up = ring(mine, 0, ROWS, f_up, 0)
-    to_dn = ring(mine, 0, ROWS, f_dn, 1)
-    to_pair = ring(mine, 0, ROWS, f_pair, 2)
-    on_up = ring(c_dn, 0, half, f_up, 3)
-    on_dn = ring(c_up, half, half, f_dn, 4)
-    pair_dn = ring(c_dn, 0, ROWS, f_pair, 5)
-    pair_up = ring(c_up, 0, ROWS, f_pair, 6)
-    pair_op_a = ring(c_op, 0, half, f_pair, 7)
-    pair_op_b = ring(c_op, half, half, f_pair, 8)
-    sent = [to_up, to_dn, to_pair, on_up, on_dn, pair_dn, pair_up, pair_op_a, pair_op_b]
-
-    def partial_copy(c):
+    sent = []
+
+    def go(copy):
+        copy.start()
+        sent.append(copy)
+
+    def partial(m, target):
+        x = label(m)
+        target[:, :HID] = jnp.dot(xall[x, :, :BLK], win_ref[...], preferred_element_type=F32)
+        target[:, HID:] = lax.dot_general(
+            xall[x, :, BLK:], wout_ref[...], NT, preferred_element_type=F32
+        )
+
+    def relay(z, h):
         return pltpu.make_async_remote_copy(
-            src_ref=part_s.at[c], dst_ref=part_r.at[i],
-            send_sem=rs_ss.at[c], recv_sem=rs_rs.at[i],
-            device_id=(e * GROUP + c, f), device_id_type=MESH,
-        )
-
-    def partial_landed(d):
+            src_ref=part_s.at[2 + 4 * z, pl.ds(h * half, half)], dst_ref=relay_r.at[z, h],
+            send_sem=rel_ss.at[2 * z + h], recv_sem=rel_rs.at[2 * z + h],
+            device_id=place(1 + 2 * h), device_id_type=MESH,
+        )
+
+    def along_x(z, h):
         return pltpu.make_async_remote_copy(
-            src_ref=part_s.at[d], dst_ref=part_r.at[d],
-            send_sem=rs_ss.at[d], recv_sem=rs_rs.at[d],
-            device_id=(e * GROUP + d, f), device_id_type=MESH,
-        )
-
-    def partials(c):
-        pre = jnp.dot(xall[c, :, :BLK], win_ref[...], preferred_element_type=F32)
-        back = lax.dot_general(xall[c, :, BLK:], wout_ref[...], NT, preferred_element_type=F32)
-
-        @pl.when(c == i)
-        def _():
-            acc[:, :HID] = pre
-            acc[:, HID:] = back
-
-        @pl.when(c != i)
-        def _():
-            part_s[c, :, :HID] = pre.astype(BF16)
-            part_s[c, :, HID:] = back.astype(BF16)
-            partial_copy(c).start()
-
-    to_up.start()
-    to_dn.start()
-    to_pair.start()
-    partials(mine)
-    ring(c_pair, 0, ROWS, f_pair, 2).wait_recv()
-    partials(c_pair)
-    ring(c_dn, 0, ROWS, f_dn, 0).wait_recv()
-    on_up.start()
-    pair_dn.start()
-    ring(c_up, 0, ROWS, f_up, 1).wait_recv()
-    on_dn.start()
-    pair_up.start()
-    partials(c_dn)
-    partials(c_up)
-    ring(chunk_of(pair_of(f_dn)), 0, ROWS, f_pair, 5).wait_recv()
-    partials(chunk_of(pair_of(f_dn)))
-    ring(c_op, 0, half, f_dn, 3).wait_recv()
-    pair_op_a.start()
-    ring(c_op, half, half, f_up, 4).wait_recv()
-    pair_op_b.start()
-    ring(chunk_of(pair_of(f_up)), 0, ROWS, f_pair, 6).wait_recv()
-    partials(chunk_of(pair_of(f_up)))
-    partials(c_op)
-    c_last = chunk_of(pair_of(f_op))
-    ring(c_last, 0, half, f_pair, 7).wait_recv()
-    ring(c_last, half, half, f_pair, 8).wait_recv()
-    partials(c_last)
-
-    for k in range(1, GROUP):
-        d = turn(i + k, GROUP)
-        partial_landed(d).wait_recv()
-        acc[...] += part_r[d].astype(F32)
+            src_ref=part_s.at[4 * z + 3 - 2 * h], dst_ref=next_r.at[z, h],
+            send_sem=nex_ss.at[2 * z + h], recv_sem=nex_rs.at[2 * z + h],
+            device_id=place(3 - 2 * h), device_id_type=MESH,
+        )
+
+    def along_z():
+        return pltpu.make_async_remote_copy(
+            src_ref=part_s.at[4], dst_ref=pair_r,
+            send_sem=par_ss.at[0], recv_sem=par_rs.at[0],
+            device_id=place(4), device_id_type=MESH,
+        )
+
+    def far(z):
+        partial(2 + 4 * z, work.at[z])
+        part_s[2 + 4 * z] = work[z].astype(BF16)
+        go(relay(z, 0))
+        go(relay(z, 1))
+
+    def near(z, h):
+        m = 4 * z + 3 - 2 * h
+        relay(z, h).wait_recv()
+        if h:
+            part_s[m, :half] = work[h, :half].astype(BF16)
+            part_s[m, half:] = (work[h, half:] + relay_r[z, h].astype(F32)).astype(BF16)
+        else:
+            part_s[m, :half] = (work[h, :half] + relay_r[z, h].astype(F32)).astype(BF16)
+            part_s[m, half:] = work[h, half:].astype(BF16)
+        go(along_x(z, h))
+
+    go(ring(mine, 0, ROWS, side(2), 0))
+    go(ring(mine, 0, ROWS, side(6), 1))
+    go(ring(mine, 0, ROWS, side(1), 2))
+    far(1)
+    ring(over(1), 0, ROWS, side(1), 2).wait_recv()
+    far(0)
+    ring(over(2), 0, ROWS, side(2), 0).wait_recv()
+    go(ring(over(2), 0, half, side(6), 3))
+    go(ring(over(2), 0, ROWS, side(1), 5))
+    ring(over(6), 0, ROWS, side(6), 1).wait_recv()
+    go(ring(over(6), half, half, side(2), 4))
+    go(ring(over(6), 0, ROWS, side(1), 6))
+    partial(7, work.at[0])
+    partial(5, work.at[1])
+    near(1, 0)
+    near(1, 1)
+    ring(over(3), 0, ROWS, side(1), 5).wait_recv()
+    partial(3, work.at[0])
+    ring(over(7), 0, ROWS, side(1), 6).wait_recv()
+    partial(1, work.at[1])
+    ring(over(4), 0, half, side(6), 3).wait_recv()
+    go(ring(over(4), 0, half, side(1), 7))
+    ring(over(4), half, half, side(2), 4).wait_recv()
+    go(ring(over(4), half, half, side(1), 8))
+    near(0, 0)
+    near(0, 1)
+    partial(4, acc.at[1])
+    ring(over(5), 0, half, side(1), 7).wait_recv()
+    ring(over(5), half, half, side(1), 8).wait_recv()
+    partial(0, acc.at[0])
+    for z in (1, 0):
+        for h in (0, 1):
+            along_x(z, h).wait_recv()
+            acc[z] += next_r[z, h].astype(F32)
+        if z:
+            part_s[4] = acc[1].astype(BF16)
+            go(along_z())
+    along_z().wait_recv()
+
+    owned = label(0)
 
     def activate(block, carry):
         rows = pl.ds(pl.multiple_of(block * 16, 16), 16)
-        act_value, act_slope = gelu_pair(acc[rows, :HID])
-        hp[i, rows, :HID] = act_value.astype(BF16)
-        hp[i, rows, HID:] = (acc[rows, HID:] * act_slope).astype(BF16)
+        total = acc[0, rows, :] + pair_r[rows, :].astype(F32)
+        act_value, act_slope = gelu_pair(total[:, :HID])
+        hp[owned, rows, :HID] = act_value.astype(BF16)
+        hp[owned, rows, HID:] = (total[:, HID:] * act_slope).astype(BF16)
         return carry
 
     lax.fori_loop(0, ROWS // 16, activate, 0)
 
-    def finished(c, target):
+    def spread(m, start, size, to, index):
+        rows = pl.ds(start, size)
         return pltpu.make_async_remote_copy(
-            src_ref=hp.at[c], dst_ref=hp.at[c],
-            send_sem=ag_ss.at[target], recv_sem=ag_rs.at[c],
-            device_id=(e * GROUP + target, f), device_id_type=MESH,
-        )
-
-    for k in range(1, GROUP):
-        finished(i, turn(i + k, GROUP)).start()
-
-    for k in range(GROUP):
-        d = turn(i + k, GROUP)
-        if k:
-            finished(d, d).wait_recv()
+            src_ref=hp.at[label(m), rows], dst_ref=hp.at[label(m), rows],
+            send_sem=ag_ss.at[index], recv_sem=ag_rs.at[index],
+            device_id=place(to), device_id_type=MESH,
+        )
+
+    def grads(m, first=False):
+        c = label(m)
         add_in = lax.dot_general(
-            xall[d, :, :BLK], hp[d, :, HID:], TN, preferred_element_type=F32
+            xall[c, :, :BLK], hp[c, :, HID:], TN, preferred_element_type=F32
         )
         add_out = lax.dot_general(
-            hp[d, :, :HID], xall[d, :, BLK:], TN, preferred_element_type=F32
-        )
-        if k:
+            hp[c, :, :HID], xall[c, :, BLK:], TN, preferred_element_type=F32
+        )
+        if first:
+            gin[...] = add_in
+            gout[...] = add_out
+        else:
             gin[...] += add_in
             gout[...] += add_out
-        else:
-            gin[...] = add_in
-            gout[...] = add_out
+
+    go(spread(0, 0, ROWS, 4, 0))
+    go(spread(0, 0, ROWS, 1, 1))
+    go(spread(0, 0, ROWS, 3, 2))
+    grads(0, True)
+    spread(4, 0, ROWS, 4, 0).wait_recv()
+    go(spread(4, 0, ROWS, 1, 3))
+    go(spread(4, 0, ROWS, 3, 4))
+    spread(1, 0, ROWS, 1, 1).wait_recv()
+    go(spread(1, 0, half, 3, 5))
+    spread(3, 0, ROWS, 3, 2).wait_recv()
+    go(spread(3, half, half, 1, 6))
+    grads(4)
+    grads(1)
+    grads(3)
+    spread(2, 0, half, 3, 5).wait_recv()
+    spread(2, half, half, 1, 6).wait_recv()
+    spread(5, 0, ROWS, 1, 3).wait_recv()
+    go(spread(5, 0, half, 3, 7))
+    spread(7, 0, ROWS, 3, 4).wait_recv()
+    go(spread(7, half, half, 1, 8))
+    grads(2)
+    grads(5)
+    grads(7)
+    spread(6, 0, half, 3, 7).wait_recv()
+    spread(6, half, half, 1, 8).wait_recv()
+    grads(6)
 
     def squares(ref, lanes, width, rows):
         def step(block, total):
@@ -418,16 +475,16 @@
 
     for copy in sent:
         copy.wait_send()
-    for k in range(1, GROUP):
-        partial_copy(turn(i + k, GROUP)).wait_send()
-        finished(i, turn(i + k, GROUP)).wait_send()
     for start, _ in over_group + over_ffn + group_norms + ffn_norms:
         start.wait_send()
 
 
 def shards(tokens, cotangent, expert_ids, in_weight, out_weight, width_states, hidden_states):
     vmem = pl.BlockSpec(memory_space=pltpu.VMEM)
-    dma8 = pltpu.SemaphoreType.DMA((8,))
+    def dma(count):
+        return pltpu.SemaphoreType.DMA((count,))
+
+    dma8 = dma(8)
     update_in, update_out = pl.pallas_call(
         kernel,
         out_shape=(
@@ -441,8 +498,11 @@
             pltpu.VMEM((EXPERTS, ROWS, 128), BF16),
             pltpu.VMEM((GROUP, ROWS, 2 * BLK), BF16),
             pltpu.VMEM((GROUP, ROWS, 2 * HID), BF16),
-            pltpu.VMEM((GROUP, ROWS, 2 * HID), BF16),
-            pltpu.VMEM((ROWS, 2 * HID), F32),
+            pltpu.VMEM((2, 2, ROWS // 2, 2 * HID), BF16),
+            pltpu.VMEM((2, 2, ROWS, 2 * HID), BF16),
+            pltpu.VMEM((ROWS, 2 * HID), BF16),
+            pltpu.VMEM((2, ROWS, 2 * HID), F32),
+            pltpu.VMEM((2, ROWS, 2 * HID), F32),
             pltpu.VMEM((GROUP, ROWS, 2 * HID), BF16),
             pltpu.VMEM((BLK, HID), F32),
             pltpu.VMEM((HID, BLK), F32),
@@ -452,9 +512,8 @@
             pltpu.VMEM((FFN, 8, BLK), F32),
             pltpu.VMEM((GROUP, 8, 128), F32),
             pltpu.VMEM((FFN, 8, 128), F32),
-            dma8, dma8,
-            pltpu.SemaphoreType.DMA((9,)), pltpu.SemaphoreType.DMA((9,)),
-            dma8, dma8, dma8, dma8, dma8, dma8, dma8, dma8, dma8, dma8, dma8, dma8,
+            dma8, dma8, dma(9), dma(9), dma(4), dma(4), dma(4), dma(4), dma(1), dma(1),
+            dma(9), dma(9), dma8, dma8, dma8, dma8, dma8, dma8, dma8, dma8,
         ],
         compiler_params=pltpu.CompilerParams(
             collective_id=0, has_side_effects=True, vmem_limit_bytes=56 * 1024 * 1024

time: 168 us -> 124 us (0.74)
  Pallas kernels: 165 us -> 120 us
    pallas_call x1, Pallas kernels: 165 us -> 120 us  [shards(): pl.pallas_call(kernel, out_shape=(jax.ShapeDtypeStruct((BLK, HID), BF16),...]
where the time goes in v2:
time: 124 us
  Pallas kernels  120 us (97%)
  local copies, waits for them, and re-layouts  2.89 us (2%)
    pallas_call x1, Pallas kernels, shards(): pl.pallas_call(kernel, out_shape=(jax.ShapeDtypeStruct((BLK, HID), BF16),...  120 us
    unnamed x4, local copies, waits for them, and re-layouts  2.89 us

profile of v2, /device:TPU:1, one launch (start us, length us, event | category | flops | bytes accessed | tf_op | source)
XLA Modules:
  0.0 123.9 jit_solution(11330826469855378864)
XLA Ops:
  0.6 120.4 %switch_update.1 = (bf16[512,640]{1,0:T(8,128)(2,1)}, bf16[640,512]{1,0:T(8,128)(2,1)}) custom-call(s32[1,128]{1,0:T(1,128)} %bitcast.9, bf16[128,4096]{1,0:T(8,128)(2,1)} %tok_ref.1, bf16[128,4096]{1,0:T(8,128)(2,1)} %cot_ref.1, bf16[512,640]{1,0:T(8,128)(2,1)} %bitcast.7, bf16[640,512]{1,0:T(8,128)(2,1)} %bitcast.8, f32[2,8,4096]{2,1,0:T(8,128)} %ws_ref.1, ...), custom_call_target="tpu_custom_call" | custom-call | tf_op jit(solution)/shard_map/switch_update/pallas_call | solution.py:488
  121.0 0.0 copy-start
  121.0 2.0 %copy.11 = bf16[1,512,640]{2,1,0:T(8,128)(2,1)} copy(bf16[1,512,640]{2,1,0:T(8,128)(2,1)} %bitcast.6) | data formatting | bytes 1310720
  123.1 0.0 copy-done
  123.1 0.8 copy.12
Async XLA Ops:
  121.0 2.1 %copy-start = (bf16[640,512]{1,0:T(8,128)(2,1)S(1)}, bf16[640,512]{1,0:T(8,128)(2,1)}, u32[]{:S(2)}) copy-start(bf16[640,512]{1,0:T(8,128)(2,1)} %get-tuple-element.5) | copy-start | bytes 1966084

commit v3 on v2

v3 whole, which is shorter than its diff:
```python
import math

import jax
import jax.numpy as jnp
from jax import lax
from jax.experimental import pallas as pl
from jax.experimental.pallas import tpu as pltpu
from jax.sharding import PartitionSpec as P

D = 4096
FF = 5120
GROUP = 8
EXPERTS = 8
FFN = 8
CAP = 20
BLK = D // GROUP
HID = FF // FFN
TOK = 128
ROWS = GROUP * CAP
PIECES = BLK // 128
SEND = PIECES * CAP

DECAY_RATE = 0.9
EPS_ONE = 1e-30
ROOT_COEF = math.sqrt(2.0 / math.pi)
CUBIC_COEF = 0.044715

MESH = pl.DeviceIdType.MESH
F32 = jnp.float32
BF16 = jnp.bfloat16
NT = (((1,), (1,)), ((), ()))
TN = (((0,), (0,)), ((), ()))


def gelu_pair(inputs):
    inner = ROOT_COEF * (inputs + CUBIC_COEF * inputs * inputs * inputs)
    tangent = jnp.tanh(inner)
    act_value = 0.5 * inputs * (1.0 + tangent)
    act_slope = 0.5 * (1.0 + tangent) + 0.5 * inputs * (1.0 - tangent * tangent) * ROOT_COEF * (
        1.0 + 3.0 * CUBIC_COEF * inputs * inputs
    )
    return (act_value, act_slope)


def iota(shape, dim):
    return lax.broadcasted_iota(jnp.int32, shape, dim)


def kernel(
    ids_any, tok_any, cot_any, win_any, wout_any, ws_any, hs_any,
    raw_in, raw_out, factor_in, factor_out,
    ids_ref, tok_ref, cot_ref, win_ref, wout_ref, ws_ref, hs_ref,
    chunk_s, chunk_r, xall, part_s, relay_r, next_r, pair_r, far_r, work, acc, slope, hp, gin, gout,
    lane_in, lane_out, stat_h, stat_w, norm_g, norm_f,
    a2a_ss, a2a_rs, ring_ss, ring_rs, rel_ss, rel_rs, nex_ss, nex_rs, par_ss, par_rs, far_ss, far_rs, ag_ss, ag_rs,
    sh_ss, sh_rs, sw_ss, sw_rs, ng_ss, ng_rs, nf_ss, nf_rs,
    load_sem, save_sem,
):
    p = lax.axis_index("expert")
    f = lax.axis_index("ffn")
    e = p // GROUP
    i = p % GROUP
    y = f // 2
    core = f % 2

    def turn(value, n):
        return lax.rem(value, n)

    def flip(value, mask):
        for bit in (1, 2, 4):
            if mask & bit:
                value = value + bit * (1 - 2 * turn(value // bit, 2))
        return value

    def xor(*values):
        total = 0
        for bit in (1, 2, 4):
            total = total + bit * turn(sum(value // bit for value in values), 2)
        return total

    turned = core * 4 + y
    mine = xor(turned, i, e)

    def label(m):
        return flip(mine, m ^ 6)

    def over(d):
        return flip(mine, (d % 2) * 4 + d // 2)

    def place(m):
        return (e * GROUP + flip(i, m), f)

    def side(d):
        return (p, flip(f, d))

    loads = [
        pltpu.make_async_copy(source, here, load_sem.at[index])
        for index, (source, here) in enumerate((
            (ids_any, ids_ref), (tok_any, tok_ref), (cot_any, cot_ref), (win_any, win_ref),
            (wout_any, wout_ref), (ws_any, ws_ref), (hs_any, hs_ref),
        ))
    ]
    for load in loads:
        load.start()

    barrier = pltpu.get_barrier_semaphore()
    for q in range(EXPERTS):
        source = q * GROUP + mine

        @pl.when(source != p)
        def _():
            pl.semaphore_signal(barrier, inc=1, device_id=(source, f), device_id_type=MESH)

    for k in range(1, GROUP):
        pl.semaphore_signal(
            barrier, inc=1, device_id=(e * GROUP + turn(i + k, GROUP), f), device_id_type=MESH
        )
        pl.semaphore_signal(barrier, inc=1, device_id=(p, turn(f + k, FFN)), device_id_type=MESH)

    loads[0].wait()
    ids = ids_ref[...]
    onehot = iota((EXPERTS, TOK), 0) == ids
    earlier = jnp.where(iota((TOK, TOK), 0) < iota((TOK, TOK), 1), 1.0, 0.0).astype(BF16)
    before = jnp.dot(
        jnp.where(onehot, 1.0, 0.0).astype(BF16), earlier, preferred_element_type=F32
    )
    slot = jnp.sum(jnp.where(onehot, before, 0.0), axis=0, keepdims=True).astype(jnp.int32)
    pieces_row = iota((SEND, PIECES * TOK), 0) - CAP * (iota((SEND, PIECES * TOK), 1) // TOK)

    def build(a, ref):
        def step(expert, carry):
            place = jnp.where(ids == expert, slot, -ROWS * 2)
            place = jnp.concatenate([place] * PIECES, axis=1)
            select = jnp.where(pieces_row == place, 1.0, 0.0).astype(BF16)
            offset = xor(turned, expert, i) * BLK
            parts = [
                ref[:, pl.ds(pl.multiple_of(offset + g * 128, 128), 128)] for g in range(PIECES)
            ]
            chunk_s[a, expert] = jnp.dot(
                select, jnp.concatenate(parts, axis=0), preferred_element_type=F32
            ).astype(BF16)
            return carry

        loads[1 + a].wait()
        lax.fori_loop(0, EXPERTS, step, 0)

    build(0, tok_ref)
    pl.semaphore_wait(barrier, EXPERTS + 2 * (GROUP - 1) - jnp.where(mine == i, 1, 0))

    def routed(a, expert):
        target = expert * GROUP + xor(turned, expert, i)
        copy = pltpu.make_async_remote_copy(
            src_ref=chunk_s.at[a, expert], dst_ref=chunk_r.at[a, e],
            send_sem=a2a_ss.at[a, expert], recv_sem=a2a_rs.at[a, e],
            device_id=(target, f), device_id_type=MESH,
        )
        return target, copy

    def route(a):
        for k in range(EXPERTS):
            target, copy = routed(a, turn(e + 4 + k, EXPERTS))

            @pl.when(target != p)
            def _():
                copy.start()

            @pl.when(target == p)
            def _():
                chunk_r[a, e] = chunk_s[a, e]

    def arrived(a):
        for q in range(EXPERTS):
            @pl.when(q * GROUP + mine != p)
            def _():
                pltpu.make_async_remote_copy(
                    src_ref=chunk_s.at[a, q], dst_ref=chunk_r.at[a, q],
                    send_sem=a2a_ss.at[a, q], recv_sem=a2a_rs.at[a, q],
                    device_id=(p, f), device_id_type=MESH,
                ).wait_recv()

    def unpack(a):
        received = chunk_r[a].reshape(EXPERTS * SEND, 128)
        row_of = iota((ROWS, EXPERTS * SEND), 0)
        source_of = lax.shift_right_logical(row_of * 3277, 16)
        gap = iota((ROWS, EXPERTS * SEND), 1) - (SEND - CAP) * source_of - row_of
        for piece in range(PIECES):
            select = jnp.where(gap == CAP * piece, 1.0, 0.0).astype(BF16)
            xall[a, mine, :, piece * 128 : (piece + 1) * 128] = jnp.dot(
                select, received, preferred_element_type=F32
            ).astype(BF16)

    def ring(a, chunk, start, size, device, index):
        rows = pl.ds(start, size)
        return pltpu.make_async_remote_copy(
            src_ref=xall.at[a, chunk, rows], dst_ref=xall.at[a, chunk, rows],
            send_sem=ring_ss.at[a, index], recv_sem=ring_rs.at[a, index],
            device_id=device, device_id_type=MESH,
        )

    half = ROWS // 2
    sent = []

    def go(copy):
        copy.start()
        sent.append(copy)

    def partial(a, m):
        x = xall[a, label(m)]
        if a:
            return lax.dot_general(x, wout_ref[...], NT, preferred_element_type=F32)
        return jnp.dot(x, win_ref[...], preferred_element_type=F32)

    def relay(a, z, h):
        return pltpu.make_async_remote_copy(
            src_ref=part_s.at[a, 2 + 4 * z, pl.ds(h * half, half)], dst_ref=relay_r.at[a, z, h],
            send_sem=rel_ss.at[a, 2 * z + h], recv_sem=rel_rs.at[a, 2 * z + h],
            device_id=place(1 + 2 * h), device_id_type=MESH,
        )

    def along_x(a, z, h):
        return pltpu.make_async_remote_copy(
            src_ref=part_s.at[a, 4 * z + 3 - 2 * h], dst_ref=next_r.at[a, z, h],
            send_sem=nex_ss.at[a, 2 * z + h], recv_sem=nex_rs.at[a, 2 * z + h],
            device_id=place(3 - 2 * h), device_id_type=MESH,
        )

    def along_z(a):
        return pltpu.make_async_remote_copy(
            src_ref=part_s.at[a, 4], dst_ref=pair_r.at[a],
            send_sem=par_ss.at[a], recv_sem=par_rs.at[a],
            device_id=place(4), device_id_type=MESH,
        )

    def far_z():
        return pltpu.make_async_remote_copy(
            src_ref=part_s.at[1, 6], dst_ref=far_r,
            send_sem=far_ss.at[0], recv_sem=far_rs.at[0],
            device_id=place(4), device_id_type=MESH,
        )

    def far(a, z):
        part_s[a, 2 + 4 * z] = partial(a, 2 + 4 * z).astype(BF16)
        go(relay(a, z, 0))
        go(relay(a, z, 1))

    def near(a, z):
        for h in (0, 1):
            work[h] = partial(a, 4 * z + 3 - 2 * h)
        for h in (0, 1):
            m = 4 * z + 3 - 2 * h
            if a and z:
                part_s[a, m] = work[h].astype(BF16)
                go(along_x(a, z, h))
                continue
            relay(a, z, h).wait_recv()
            met, other = pl.ds(h * half, half), pl.ds((1 - h) * half, half)
            part_s[a, m, other] = work[h, other].astype(BF16)
            part_s[a, m, met] = (work[h, met] + relay_r[a, z, h].astype(F32)).astype(BF16)
            go(along_x(a, z, h))

    def ring_open(a):
        go(ring(a, mine, 0, ROWS, side(2), 0))
        go(ring(a, mine, 0, ROWS, side(6), 1))
        go(ring(a, mine, 0, ROWS, side(1), 2))

    def ring_pass(a):
        ring(a, over(2), 0, ROWS, side(2), 0).wait_recv()
        go(ring(a, over(2), 0, half, side(6), 3))
        go(ring(a, over(2), 0, ROWS, side(1), 5))
        ring(a, over(6), 0, ROWS, side(6), 1).wait_recv()
        go(ring(a, over(6), half, half, side(2), 4))
        go(ring(a, over(6), 0, ROWS, side(1), 6))

    def ring_halves(a):
        ring(a, over(4), 0, half, side(6), 3).wait_recv()
        go(ring(a, over(4), 0, half, side(1), 7))
        ring(a, over(4), half, half, side(2), 4).wait_recv()
        go(ring(a, over(4), half, half, side(1), 8))

    def far_pair(a):
        ring(a, over(1), 0, ROWS, side(1), 2).wait_recv()
        far(a, 0)

    def near_pair(a):
        ring(a, over(3), 0, ROWS, side(1), 5).wait_recv()
        ring(a, over(7), 0, ROWS, side(1), 6).wait_recv()
        near(a, 0)

    def own_column(a):
        acc[a, 1] = partial(a, 4)
        ring(a, over(5), 0, half, side(1), 7).wait_recv()
        ring(a, over(5), half, half, side(1), 8).wait_recv()
        acc[a, 0] = partial(a, 0)

    def sum_x(a, z):
        along_x(a, z, 0).wait_recv()
        along_x(a, z, 1).wait_recv()
        total = acc[a, z] + next_r[a, z, 0].astype(F32) + next_r[a, z, 1].astype(F32)
        if z:
            part_s[a, 4] = total.astype(BF16)
            go(along_z(a))
        else:
            acc[a, 0] = total

    route(0)
    build(1, cot_ref)
    arrived(0)
    route(1)
    unpack(0)
    ring_open(0)
    for load in loads[3:]:
        load.wait()
    far(0, 1)
    far_pair(0)
    ring_pass(0)
    near(0, 1)
    near_pair(0)
    ring_halves(0)
    arrived(1)
    unpack(1)
    ring_open(1)
    part_s[1, 6] = partial(1, 6).astype(BF16)
    go(far_z())
    own_column(0)
    sum_x(0, 1)
    ring(1, over(1), 0, ROWS, side(1), 2).wait_recv()
    work[0] = partial(1, 2)
    ring_pass(1)
    far_z().wait_recv()
    part_s[1, 2] = (work[0] + far_r[...].astype(F32)).astype(BF16)
    go(relay(1, 0, 0))
    go(relay(1, 0, 1))
    near(1, 1)
    ring_halves(1)
    sum_x(0, 0)
    along_z(0).wait_recv()

    owned = label(0)

    def activate(block, carry):
        rows = pl.ds(pl.multiple_of(block * 16, 16), 16)
        act_value, act_slope = gelu_pair(acc[0, 0, rows, :] + pair_r[0, rows, :].astype(F32))
        hp[0, owned, rows, :] = act_value.astype(BF16)
        slope[rows, :] = act_slope
        return carry

    def backward(block, carry):
        rows = pl.ds(pl.multiple_of(block * 16, 16), 16)
        back = acc[1, 0, rows, :] + pair_r[1, rows, :].astype(F32)
        hp[1, owned, rows, :] = (back * slope[rows, :]).astype(BF16)
        return carry

    def spread(a, m, start, size, to, index):
        rows = pl.ds(start, size)
        return pltpu.make_async_remote_copy(
            src_ref=hp.at[a, label(m), rows], dst_ref=hp.at[a, label(m), rows],
            send_sem=ag_ss.at[a, index], recv_sem=ag_rs.at[a, index],
            device_id=place(to), device_id_type=MESH,
        )

    def open_spread(a):
        go(spread(a, 0, 0, ROWS, 4, 0))
        go(spread(a, 0, 0, ROWS, 1, 1))
        go(spread(a, 0, 0, ROWS, 3, 2))

    def pass_pair(a):
        spread(a, 4, 0, ROWS, 4, 0).wait_recv()
        go(spread(a, 4, 0, ROWS, 1, 3))
        go(spread(a, 4, 0, ROWS, 3, 4))

    def pass_next(a):
        spread(a, 1, 0, ROWS, 1, 1).wait_recv()
        go(spread(a, 1, 0, half, 3, 5))
        spread(a, 3, 0, ROWS, 3, 2).wait_recv()
        go(spread(a, 3, half, half, 1, 6))

    def wait_far(a):
        spread(a, 2, 0, half, 3, 5).wait_recv()
        spread(a, 2, half, half, 1, 6).wait_recv()

    def pass_pair_next(a):
        spread(a, 5, 0, ROWS, 1, 3).wait_recv()
        go(spread(a, 5, 0, half, 3, 7))
        spread(a, 7, 0, ROWS, 3, 4).wait_recv()
        go(spread(a, 7, half, half, 1, 8))

    def wait_pair_far(a):
        spread(a, 6, 0, half, 3, 7).wait_recv()
        spread(a, 6, half, half, 1, 8).wait_recv()

    def grads(a, m, first=False):
        c = label(m)
        if a:
            add, total = lax.dot_general(
                xall[0, c], hp[1, c], TN, preferred_element_type=F32
            ), gin
        else:
            add, total = lax.dot_general(
                hp[0, c], xall[1, c], TN, preferred_element_type=F32
            ), gout
        if first:
            total[...] = add
        else:
            total[...] += add

    lax.fori_loop(0, ROWS // 16, activate, 0)
    open_spread(0)
    near_pair(1)
    own_column(1)
    sum_x(1, 1)
    pass_pair(0)
    sum_x(1, 0)
    along_z(1).wait_recv()
    lax.fori_loop(0, ROWS // 16, backward, 0)
    open_spread(1)
    grads(0, 0, True)
    grads(0, 4)
    pass_next(0)
    pass_pair(1)
    grads(0, 1)
    grads(0, 3)
    wait_far(0)
    go(spread(0, 2, 0, ROWS, 4, 7))
    grads(0, 2)
    pass_next(1)
    spread(0, 5, 0, ROWS, 1, 3).wait_recv()
    grads(0, 5)
    spread(0, 7, 0, ROWS, 3, 4).wait_recv()
    grads(0, 7)
    grads(1, 0, True)
    grads(1, 4)
    grads(1, 1)
    grads(1, 3)
    pass_pair_next(1)
    grads(1, 5)
    grads(1, 7)
    spread(0, 6, 0, ROWS, 4, 7).wait_recv()
    grads(0, 6)
    wait_far(1)
    grads(1, 2)

    def squares(ref, lanes, width, rows):
        def step(block, total):
            here = pl.ds(pl.multiple_of(block * 32, 32), 32)
            value = ref[here, :]
            value = value * value + EPS_ONE
            folded = value[:, :128]
            for g in range(1, width // 128):
                folded = folded + value[:, g * 128 : (g + 1) * 128]
            lanes[here, :] = folded
            return total + jnp.sum(value.reshape(4, 8, width), axis=0)

        total = lax.fori_loop(0, rows // 32, step, jnp.zeros((8, width), F32))
        return jnp.sum(total, axis=0, keepdims=True), jnp.sum(lanes[...].T, axis=0, keepdims=True)

    hidden_prev = hs_ref[:, pl.ds(e, 1), :]
    width_prev = ws_ref[:, pl.ds(e, 1), pl.ds(pl.multiple_of(i * BLK, BLK), BLK)]

    def exchange(at, own, ssem, rsem, device):
        copies = []
        for k in range(1, 8):
            d = turn(own + k, 8)
            copies.append((
                pltpu.make_async_remote_copy(
                    src_ref=at(own), dst_ref=at(own),
                    send_sem=ssem(d), recv_sem=rsem(own),
                    device_id=device(d), device_id_type=MESH,
                ),
                pltpu.make_async_remote_copy(
                    src_ref=at(d), dst_ref=at(d),
                    send_sem=ssem(d), recv_sem=rsem(d),
                    device_id=device(d), device_id_type=MESH,
                ),
            ))
        return copies

    def in_group(d):
        return (e * GROUP + d, f)

    def in_ffn(d):
        return (p, d)

    def both(a):
        return exchange(
            lambda d: stat_h.at[a, d], i, lambda d: sh_ss.at[a, d], lambda d: sh_rs.at[a, d],
            in_group,
        ) + exchange(
            lambda d: stat_w.at[a, d], f, lambda d: sw_ss.at[a, d], lambda d: sw_rs.at[a, d],
            in_ffn,
        )

    stats = [both(0), both(1)]

    cols_out, rows_out = squares(gout, lane_out, BLK, HID)
    hidden_sum = jnp.sum(hidden_prev[1], axis=1, keepdims=True)
    stat_h[0, i] = jnp.broadcast_to(rows_out, (8, HID))
    stat_w[0, f] = jnp.concatenate([cols_out, jnp.broadcast_to(hidden_sum, (7, BLK))], axis=0)
    for start, _ in stats[0]:
        start.start()

    wait_pair_far(1)
    grads(1, 6)
    cols_in, rows_in = squares(gin, lane_in, HID, BLK)
    stat_h[1, i] = jnp.broadcast_to(cols_in, (8, HID))
    stat_w[1, f] = jnp.broadcast_to(rows_in, (8, BLK))
    for start, _ in stats[1]:
        start.start()

    def scaled(ref, lanes, scale, width, rows):
        def step(block, total):
            here = pl.ds(pl.multiple_of(block * 32, 32), 32)
            factor = lanes[here, :]
            for g in range(width // 128):
                cols = slice(g * 128, (g + 1) * 128)
                value = ref[here, cols] * factor * scale[:, cols]
                ref[here, cols] = value
                total = total + jnp.sum((value * value).reshape(4, 8, 128), axis=0)
            return total

        total = lax.fori_loop(0, rows // 32, step, jnp.zeros((8, 128), F32))
        return jnp.sum(total, axis=0, keepdims=True)

    for _, arrival in stats[0]:
        arrival.wait_recv()
    sum_out = jnp.sum(stat_w[0], axis=0)
    rows_out = DECAY_RATE * hidden_prev[1] + (1.0 - DECAY_RATE) * (
        jnp.sum(stat_h[0], axis=0)[0:1] / D
    )
    cols_out = DECAY_RATE * width_prev[1] + (1.0 - DECAY_RATE) * sum_out[0:1] / FF
    lane_out[...] = jnp.broadcast_to(lax.rsqrt(rows_out), (128, HID)).T
    norm_out = scaled(gout, lane_out, lax.rsqrt(cols_out), BLK, HID)
    save_out = pltpu.make_async_copy(gout, raw_out, save_sem.at[0])
    save_out.start()

    for _, arrival in stats[1]:
        arrival.wait_recv()
    sum_in = jnp.sum(stat_w[1], axis=0)
    cols_in = DECAY_RATE * hidden_prev[0] + (1.0 - DECAY_RATE) * (
        jnp.sum(stat_h[1], axis=0)[0:1] / D
    )
    rows_in = DECAY_RATE * width_prev[0] + (1.0 - DECAY_RATE) * sum_in[0:1] / FF
    lane_in[...] = jnp.broadcast_to(lax.rsqrt(rows_in), (128, BLK)).T
    norm_in = scaled(gin, lane_in, lax.rsqrt(cols_in), HID, BLK)
    save_in = pltpu.make_async_copy(gin, raw_in, save_sem.at[1])
    save_in.start()

    def fold(row):
        total = row[:, :128]
        for g in range(1, row.shape[1] // 128):
            total = total + row[:, g * 128 : (g + 1) * 128]
        return total

    norm_g[i] = jnp.concatenate(
        [norm_in, norm_out, fold(sum_in[0:1]), fold(sum_out[0:1]), jnp.zeros((4, 128), F32)], axis=0
    )
    group_norms = exchange(
        lambda d: norm_g.at[d], i, lambda d: ng_ss.at[d], lambda d: ng_rs.at[d], in_group
    )
    for start, _ in group_norms:
        start.start()
    for _, arrival in group_norms:
        arrival.wait_recv()
    group_sum = jnp.sum(norm_g[...], axis=0)
    norm_f[f] = group_sum
    ffn_norms = exchange(
        lambda d: norm_f.at[d], f, lambda d: nf_ss.at[d], lambda d: nf_rs.at[d], in_ffn
    )
    for start, _ in ffn_norms:
        start.start()
    for _, arrival in ffn_norms:
        arrival.wait_recv()
    norm_sum = jnp.sum(jnp.sum(norm_f[...], axis=0), axis=1, keepdims=True)
    totals = jnp.sum(group_sum, axis=1, keepdims=True)

    whole_count = float(D) * float(FF)
    width_mean = jnp.sum(ws_ref[0, pl.ds(e, 1), :], axis=1, keepdims=True) / D
    mean_in = DECAY_RATE * width_mean + (1.0 - DECAY_RATE) * totals[2:3] / whole_count
    mean_out = (
        DECAY_RATE * sum_out[1:2, 0:1] / FF + (1.0 - DECAY_RATE) * totals[3:4] / whole_count
    )
    def last_factor(mean, norm):
        return jnp.sqrt(mean) / jnp.maximum(1.0, jnp.sqrt(mean * (norm / whole_count)))

    factor_in[...] = last_factor(mean_in, norm_sum[0:1])
    factor_out[...] = last_factor(mean_out, norm_sum[1:2])

    save_in.wait()
    save_out.wait()
    for a in range(2):
        for q in range(EXPERTS):
            target, copy = routed(a, q)

            @pl.when(target != p)
            def _():
                copy.wait_send()

    for copy in sent:
        copy.wait_send()
    for start, _ in stats[0] + stats[1] + group_norms + ffn_norms:
        start.wait_send()


def shards(tokens, cotangent, expert_ids, in_weight, out_weight, width_states, hidden_states):
    vmem = pl.BlockSpec(memory_space=pltpu.VMEM)
    anywhere = pl.BlockSpec(memory_space=pl.ANY)

    def dma(*shape):
        return pltpu.SemaphoreType.DMA(shape)

    operands = (
        expert_ids.reshape(1, TOK), tokens, cotangent, in_weight[0], out_weight[0],
        width_states, hidden_states,
    )
    raw_in, raw_out, factor_in, factor_out = pl.pallas_call(
        kernel,
        out_shape=(
            jax.ShapeDtypeStruct((BLK, HID), F32),
            jax.ShapeDtypeStruct((HID, BLK), F32),
            jax.ShapeDtypeStruct((1, 1), F32),
            jax.ShapeDtypeStruct((1, 1), F32),
        ),
        in_specs=[anywhere] * 7,
        out_specs=(anywhere, anywhere, vmem, vmem),
        scratch_shapes=[pltpu.VMEM(value.shape, value.dtype) for value in operands]
        + [
            pltpu.VMEM((2, EXPERTS, SEND, 128), BF16),
            pltpu.VMEM((2, EXPERTS, SEND, 128), BF16),
            pltpu.VMEM((2, GROUP, ROWS, BLK), BF16),
            pltpu.VMEM((2, GROUP, ROWS, HID), BF16),
            pltpu.VMEM((2, 2, 2, ROWS // 2, HID), BF16),
            pltpu.VMEM((2, 2, 2, ROWS, HID), BF16),
            pltpu.VMEM((2, ROWS, HID), BF16),
            pltpu.VMEM((ROWS, HID), BF16),
            pltpu.VMEM((2, ROWS, HID), F32),
            pltpu.VMEM((2, 2, ROWS, HID), F32),
            pltpu.VMEM((ROWS, HID), F32),
            pltpu.VMEM((2, GROUP, ROWS, HID), BF16),
            pltpu.VMEM((BLK, HID), F32),
            pltpu.VMEM((HID, BLK), F32),
            pltpu.VMEM((BLK, 128), F32),
            pltpu.VMEM((HID, 128), F32),
            pltpu.VMEM((2, GROUP, 8, HID), F32),
            pltpu.VMEM((2, FFN, 8, BLK), F32),
            pltpu.VMEM((GROUP, 8, 128), F32),
            pltpu.VMEM((FFN, 8, 128), F32),
            dma(2, 8), dma(2, 8), dma(2, 9), dma(2, 9), dma(2, 4), dma(2, 4), dma(2, 4),
            dma(2, 4), dma(2), dma(2), dma(1), dma(1), dma(2, 9), dma(2, 9),
            dma(2, 8), dma(2, 8), dma(2, 8), dma(2, 8), dma(8), dma(8), dma(8), dma(8),
            dma(7), dma(2),
        ],
        compiler_params=pltpu.CompilerParams(
            collective_id=0, has_side_effects=True, vmem_limit_bytes=56 * 1024 * 1024
        ),
        name="switch_update",
    )(*operands)
    update_in = (raw_in * factor_in).astype(BF16)
    update_out = (raw_out * factor_out).astype(BF16)
    return (update_in[None], update_out[None])


def solution(mesh):
    return jax.shard_map(
        shards,
        mesh=mesh,
        in_specs=(
            P("expert", None),
            P("expert", None),
            P("expert", None),
            P("expert", None, "ffn"),
            P("expert", "ffn", None),
            P(),
            P(None, None, "ffn"),
        ),
        out_specs=(P("expert", None, "ffn"), P("expert", "ffn", None)),
        check_vma=False,
    )
```

time: 124 us -> 107 us (0.86)
  Pallas kernels: 120 us -> 101 us
  other arithmetic: 0 us -> 4.56 us
  local copies, waits for them, and re-layouts: 2.89 us -> 0.01 us
    pallas_call x1, Pallas kernels: 120 us -> 101 us  [shards(): pl.pallas_call(kernel, out_shape=(jax.ShapeDtypeStruct((BLK, HID), F32),...]
    broadcast_in_dim x0 -> x2, other arithmetic: none -> 4.56 us  [shards(): return (update_in[None], update_out[None])]
    unnamed x4 -> x2, local copies, waits for them, and re-layouts: 2.89 us -> 0.01 us
where the time goes in v3:
time: 107 us
  Pallas kernels  101 us (94%)
  other arithmetic  4.56 us (4%)
    pallas_call x1, Pallas kernels, shards(): pl.pallas_call(kernel, out_shape=(jax.ShapeDtypeStruct((BLK, HID), F32),...  101 us
    broadcast_in_dim x2, other arithmetic, shards(): return (update_in[None], update_out[None])  4.56 us

profile of v3, /device:TPU:1, one launch (start us, length us, event | category | flops | bytes accessed | tf_op | source)
XLA Modules:
  0.0 106.7 jit_solution(11241595653974736648)
XLA Ops:
  0.6 101.4 %switch_update.1 = (f32[512,640]{1,0:T(8,128)}, f32[640,512]{1,0:T(8,128)}, f32[1,1]{1,0:T(1,128)}, f32[1,1]{1,0:T(1,128)}) custom-call(s32[1,128]{1,0:T(1,128)} %bitcast.11, bf16[128,4096]{1,0:T(8,128)(2,1)} %tok_any.1, bf16[128,4096]{1,0:T(8,128)(2,1)} %cot_any.1, bf16[512,640]{1,0:T(8,128)(2,1)} %bitcast.9, bf16[640,512]{1,0:T(8,128)(2,1)} %bitcast.10, ...), custom_call_target="tpu_custom_call" | custom-call | tf_op jit(solution)/shard_map/switch_update/pallas_call | solution.py:614
  102.1 0.0 copy-start
  102.1 2.9 %fusion = bf16[1,512,640]{2,1,0:T(8,128)(2,1)} fusion(f32[512,640]{1,0:T(8,128)} %get-tuple-element.6, f32[]{:T(128)} %bitcast.3), kind=kLoop, calls=%fused_computation.2 | loop fusion | flops 655360 | bytes 1966084 | tf_op jit(solution)/shard_map/broadcast_in_dim | solution.py:658
  105.0 0.0 copy-done
  105.0 1.7 %fusion.1 = bf16[1,640,512]{2,1,0:T(8,128)(2,1)} fusion(f32[640,512]{1,0:T(8,128)S(1)} %copy-done, f32[]{:T(128)} %bitcast.5), kind=kLoop, calls=%fused_computation.3 | loop fusion | flops 655360 | bytes 1966084 | tf_op jit(solution)/shard_map/broadcast_in_dim | solution.py:658
Async XLA Ops:
  102.1 2.9 %copy-start = (f32[640,512]{1,0:T(8,128)S(1)}, f32[640,512]{1,0:T(8,128)}, u32[]{:S(2)}) copy-start(f32[640,512]{1,0:T(8,128)} %get-tuple-element.8) | copy-start | bytes 3932164

commit v4 on v3

--- a/solution.py
+++ b/solution.py
@@ -19,6 +19,7 @@
 ROWS = GROUP * CAP
 PIECES = BLK // 128
 SEND = PIECES * CAP
+SPLIT = 4
 
 DECAY_RATE = 0.9
 EPS_ONE = 1e-30
@@ -48,10 +49,10 @@
 
 def kernel(
     ids_any, tok_any, cot_any, win_any, wout_any, ws_any, hs_any,
-    raw_in, raw_out, factor_in, factor_out,
+    raw_in, raw_out, factors,
     ids_ref, tok_ref, cot_ref, win_ref, wout_ref, ws_ref, hs_ref,
     chunk_s, chunk_r, xall, part_s, relay_r, next_r, pair_r, far_r, work, acc, slope, hp, gin, gout,
-    lane_in, lane_out, stat_h, stat_w, norm_g, norm_f,
+    lane_in, lane_out, stat_h, stat_w, norm_g, norm_f, factor_own,
     a2a_ss, a2a_rs, ring_ss, ring_rs, rel_ss, rel_rs, nex_ss, nex_rs, par_ss, par_rs, far_ss, far_rs, ag_ss, ag_rs,
     sh_ss, sh_rs, sw_ss, sw_rs, ng_ss, ng_rs, nf_ss, nf_rs,
     load_sem, save_sem,
@@ -100,9 +101,6 @@
             (wout_any, wout_ref), (ws_any, ws_ref), (hs_any, hs_ref),
         ))
     ]
-    for load in loads:
-        load.start()
-
     barrier = pltpu.get_barrier_semaphore()
     for q in range(EXPERTS):
         source = q * GROUP + mine
@@ -116,6 +114,9 @@
             barrier, inc=1, device_id=(e * GROUP + turn(i + k, GROUP), f), device_id_type=MESH
         )
         pl.semaphore_signal(barrier, inc=1, device_id=(p, turn(f + k, FFN)), device_id_type=MESH)
+
+    for load in loads:
+        load.start()
 
     loads[0].wait()
     ids = ids_ref[...]
@@ -127,11 +128,32 @@
     slot = jnp.sum(jnp.where(onehot, before, 0.0), axis=0, keepdims=True).astype(jnp.int32)
     pieces_row = iota((SEND, PIECES * TOK), 0) - CAP * (iota((SEND, PIECES * TOK), 1) // TOK)
 
-    def build(a, ref):
-        def step(expert, carry):
-            place = jnp.where(ids == expert, slot, -ROWS * 2)
-            place = jnp.concatenate([place] * PIECES, axis=1)
-            select = jnp.where(pieces_row == place, 1.0, 0.0).astype(BF16)
+    def routed(a, expert):
+        target = expert * GROUP + xor(turned, expert, i)
+        copy = pltpu.make_async_remote_copy(
+            src_ref=chunk_s.at[a, expert], dst_ref=chunk_r.at[a, e],
+            send_sem=a2a_ss.at[a, expert], recv_sem=a2a_rs.at[a, e],
+            device_id=(target, f), device_id_type=MESH,
+        )
+        return target, copy
+
+    def send(a, expert):
+        target, copy = routed(a, expert)
+
+        @pl.when(target != p)
+        def _():
+            copy.start()
+
+        @pl.when(target == p)
+        def _():
+            chunk_r[a, e] = chunk_s[a, e]
+
+    def route(a, ref):
+        loads[1 + a].wait()
+        for expert in range(EXPERTS):
+            spot = jnp.where(ids == expert, slot, -ROWS * 2)
+            spot = jnp.concatenate([spot] * PIECES, axis=1)
+            select = jnp.where(pieces_row == spot, 1.0, 0.0).astype(BF16)
             offset = xor(turned, expert, i) * BLK
             parts = [
                 ref[:, pl.ds(pl.multiple_of(offset + g * 128, 128), 128)] for g in range(PIECES)
@@ -139,34 +161,13 @@
             chunk_s[a, expert] = jnp.dot(
                 select, jnp.concatenate(parts, axis=0), preferred_element_type=F32
             ).astype(BF16)
-            return carry
-
-        loads[1 + a].wait()
-        lax.fori_loop(0, EXPERTS, step, 0)
-
-    build(0, tok_ref)
-    pl.semaphore_wait(barrier, EXPERTS + 2 * (GROUP - 1) - jnp.where(mine == i, 1, 0))
-
-    def routed(a, expert):
-        target = expert * GROUP + xor(turned, expert, i)
-        copy = pltpu.make_async_remote_copy(
-            src_ref=chunk_s.at[a, expert], dst_ref=chunk_r.at[a, e],
-            send_sem=a2a_ss.at[a, expert], recv_sem=a2a_rs.at[a, e],
-            device_id=(target, f), device_id_type=MESH,
-        )
-        return target, copy
-
-    def route(a):
-        for k in range(EXPERTS):
-            target, copy = routed(a, turn(e + 4 + k, EXPERTS))
-
-            @pl.when(target != p)
-            def _():
-                copy.start()
-
-            @pl.when(target == p)
-            def _():
-                chunk_r[a, e] = chunk_s[a, e]
+            if not a and not expert:
+                pl.semaphore_wait(
+                    barrier, EXPERTS + 2 * (GROUP - 1) - jnp.where(mine == i, 1, 0)
+                )
+            if expert:
+                send(a, expert - 1)
+        send(a, EXPERTS - 1)
 
     def arrived(a):
         for q in range(EXPERTS):
@@ -302,10 +303,9 @@
         else:
             acc[a, 0] = total
 
-    route(0)
-    build(1, cot_ref)
+    route(0, tok_ref)
+    route(1, cot_ref)
     arrived(0)
-    route(1)
     unpack(0)
     ring_open(0)
     for load in loads[3:]:
@@ -314,13 +314,13 @@
     far_pair(0)
     ring_pass(0)
     near(0, 1)
-    near_pair(0)
-    ring_halves(0)
     arrived(1)
     unpack(1)
     ring_open(1)
     part_s[1, 6] = partial(1, 6).astype(BF16)
     go(far_z())
+    near_pair(0)
+    ring_halves(0)
     own_column(0)
     sum_x(0, 1)
     ring(1, over(1), 0, ROWS, side(1), 2).wait_recv()
@@ -332,6 +332,8 @@
     go(relay(1, 0, 1))
     near(1, 1)
     ring_halves(1)
+    near_pair(1)
+    own_column(1)
     sum_x(0, 0)
     along_z(0).wait_recv()
 
@@ -405,52 +407,56 @@
 
     lax.fori_loop(0, ROWS // 16, activate, 0)
     open_spread(0)
-    near_pair(1)
-    own_column(1)
     sum_x(1, 1)
-    pass_pair(0)
     sum_x(1, 0)
     along_z(1).wait_recv()
     lax.fori_loop(0, ROWS // 16, backward, 0)
     open_spread(1)
     grads(0, 0, True)
-    grads(0, 4)
-    pass_next(0)
-    pass_pair(1)
+    spread(0, 1, 0, ROWS, 1, 1).wait_recv()
+    go(spread(0, 1, 0, half, 3, 5))
+    spread(0, 3, 0, ROWS, 3, 2).wait_recv()
+    go(spread(0, 3, half, half, 1, 6))
+    go(spread(0, 1, 0, ROWS, 4, 3))
+    go(spread(0, 3, 0, ROWS, 4, 4))
     grads(0, 1)
     grads(0, 3)
+    spread(0, 4, 0, ROWS, 4, 0).wait_recv()
+    grads(0, 4)
+    pass_pair(1)
+    pass_next(1)
     wait_far(0)
     go(spread(0, 2, 0, ROWS, 4, 7))
     grads(0, 2)
-    pass_next(1)
-    spread(0, 5, 0, ROWS, 1, 3).wait_recv()
-    grads(0, 5)
-    spread(0, 7, 0, ROWS, 3, 4).wait_recv()
-    grads(0, 7)
     grads(1, 0, True)
     grads(1, 4)
     grads(1, 1)
     grads(1, 3)
+    spread(0, 5, 0, ROWS, 4, 3).wait_recv()
+    grads(0, 5)
     pass_pair_next(1)
     grads(1, 5)
     grads(1, 7)
+    spread(0, 7, 0, ROWS, 4, 4).wait_recv()
+    grads(0, 7)
+    wait_far(1)
+    grads(1, 2)
     spread(0, 6, 0, ROWS, 4, 7).wait_recv()
     grads(0, 6)
-    wait_far(1)
-    grads(1, 2)
 
     def squares(ref, lanes, width, rows):
         def step(block, total):
-            here = pl.ds(pl.multiple_of(block * 32, 32), 32)
-            value = ref[here, :]
-            value = value * value + EPS_ONE
-            folded = value[:, :128]
-            for g in range(1, width // 128):
-                folded = folded + value[:, g * 128 : (g + 1) * 128]
+            here = pl.ds(pl.multiple_of(block * 64, 64), 64)
+            folded, sums = None, []
+            for g in range(width // 128):
+                value = ref[here, g * 128 : (g + 1) * 128]
+                value = value * value + EPS_ONE
+                folded = value if folded is None else folded + value
+                sums.append(jnp.sum(value.reshape(8, 8, 128), axis=0))
             lanes[here, :] = folded
-            return total + jnp.sum(value.reshape(4, 8, width), axis=0)
-
-        total = lax.fori_loop(0, rows // 32, step, jnp.zeros((8, width), F32))
+            return total + jnp.concatenate(sums, axis=1)
+
+        total = lax.fori_loop(0, rows // 64, step, jnp.zeros((8, width), F32))
         return jnp.sum(total, axis=0, keepdims=True), jnp.sum(lanes[...].T, axis=0, keepdims=True)
 
     hidden_prev = hs_ref[:, pl.ds(e, 1), :]
@@ -508,16 +514,16 @@
 
     def scaled(ref, lanes, scale, width, rows):
         def step(block, total):
-            here = pl.ds(pl.multiple_of(block * 32, 32), 32)
+            here = pl.ds(pl.multiple_of(block * 64, 64), 64)
             factor = lanes[here, :]
             for g in range(width // 128):
                 cols = slice(g * 128, (g + 1) * 128)
                 value = ref[here, cols] * factor * scale[:, cols]
                 ref[here, cols] = value
-                total = total + jnp.sum((value * value).reshape(4, 8, 128), axis=0)
+                total = total + jnp.sum((value * value).reshape(8, 8, 128), axis=0)
             return total
 
-        total = lax.fori_loop(0, rows // 32, step, jnp.zeros((8, 128), F32))
+        total = lax.fori_loop(0, rows // 64, step, jnp.zeros((8, 128), F32))
         return jnp.sum(total, axis=0, keepdims=True)
 
     for _, arrival in stats[0]:
@@ -581,11 +587,19 @@
     def last_factor(mean, norm):
         return jnp.sqrt(mean) / jnp.maximum(1.0, jnp.sqrt(mean * (norm / whole_count)))
 
-    factor_in[...] = last_factor(mean_in, norm_sum[0:1])
-    factor_out[...] = last_factor(mean_out, norm_sum[1:2])
+    factor_own[...] = jnp.concatenate(
+        [
+            jnp.broadcast_to(last_factor(mean_in, norm_sum[0:1]), (4, 128)),
+            jnp.broadcast_to(last_factor(mean_out, norm_sum[1:2]), (4, 128)),
+        ],
+        axis=0,
+    )
+    save_factors = pltpu.make_async_copy(factor_own, factors, save_sem.at[2])
+    save_factors.start()
 
     save_in.wait()
     save_out.wait()
+    save_factors.wait()
     for a in range(2):
         for q in range(EXPERTS):
             target, copy = routed(a, q)
@@ -600,8 +614,36 @@
         start.wait_send()
 
 
+def finish(
+    raw_in, raw_out, factors, update_in, update_out,
+    in_f32, out_f32, in_bf16, out_bf16, factor_own, load_sem, save_sem,
+):
+    first = pltpu.make_async_copy(factors, factor_own, load_sem.at[2 * SPLIT])
+    first.start()
+    parts = []
+    for k in range(SPLIT):
+        for j, (raw, held, done, update) in enumerate((
+            (raw_in, in_f32, in_bf16, update_in), (raw_out, out_f32, out_bf16, update_out)
+        )):
+            rows = raw.shape[0] // SPLIT
+            here = pl.ds(k * rows, rows)
+            load = pltpu.make_async_copy(raw.at[here], held.at[here], load_sem.at[2 * k + j])
+            load.start()
+            save = pltpu.make_async_copy(done.at[here], update.at[here], save_sem.at[2 * k + j])
+            parts.append((4 * j, here, held, done, load, save))
+    first.wait()
+    for row, here, held, done, load, save in parts:
+        factor = factor_own[row : row + 1, :]
+        load.wait()
+        for g in range(held.shape[1] // 128):
+            cols = slice(g * 128, (g + 1) * 128)
+            done[here, cols] = (held[here, cols] * factor).astype(BF16)
+        save.start()
+    for _, _, _, _, _, save in parts:
+        save.wait()
+
+
 def shards(tokens, cotangent, expert_ids, in_weight, out_weight, width_states, hidden_states):
-    vmem = pl.BlockSpec(memory_space=pltpu.VMEM)
     anywhere = pl.BlockSpec(memory_space=pl.ANY)
 
     def dma(*shape):
@@ -611,16 +653,15 @@
         expert_ids.reshape(1, TOK), tokens, cotangent, in_weight[0], out_weight[0],
         width_states, hidden_states,
     )
-    raw_in, raw_out, factor_in, factor_out = pl.pallas_call(
+    raw_in, raw_out, factors = pl.pallas_call(
         kernel,
         out_shape=(
             jax.ShapeDtypeStruct((BLK, HID), F32),
             jax.ShapeDtypeStruct((HID, BLK), F32),
-            jax.ShapeDtypeStruct((1, 1), F32),
-            jax.ShapeDtypeStruct((1, 1), F32),
+            jax.ShapeDtypeStruct((8, 128), F32),
         ),
         in_specs=[anywhere] * 7,
-        out_specs=(anywhere, anywhere, vmem, vmem),
+        out_specs=(anywhere, anywhere, anywhere),
         scratch_shapes=[pltpu.VMEM(value.shape, value.dtype) for value in operands]
         + [
             pltpu.VMEM((2, EXPERTS, SEND, 128), BF16),
@@ -643,18 +684,33 @@
             pltpu.VMEM((2, FFN, 8, BLK), F32),
             pltpu.VMEM((GROUP, 8, 128), F32),
             pltpu.VMEM((FFN, 8, 128), F32),
+            pltpu.VMEM((8, 128), F32),
             dma(2, 8), dma(2, 8), dma(2, 9), dma(2, 9), dma(2, 4), dma(2, 4), dma(2, 4),
             dma(2, 4), dma(2), dma(2), dma(1), dma(1), dma(2, 9), dma(2, 9),
             dma(2, 8), dma(2, 8), dma(2, 8), dma(2, 8), dma(8), dma(8), dma(8), dma(8),
-            dma(7), dma(2),
+            dma(7), dma(3),
         ],
         compiler_params=pltpu.CompilerParams(
             collective_id=0, has_side_effects=True, vmem_limit_bytes=56 * 1024 * 1024
         ),
         name="switch_update",
     )(*operands)
-    update_in = (raw_in * factor_in).astype(BF16)
-    update_out = (raw_out * factor_out).astype(BF16)
+    update_in, update_out = pl.pallas_call(
+        finish,
+        out_shape=(
+            jax.ShapeDtypeStruct((BLK, HID), BF16),
+            jax.ShapeDtypeStruct((HID, BLK), BF16),
+        ),
+        in_specs=[anywhere] * 3,
+        out_specs=(anywhere, anywhere),
+        scratch_shapes=[
+            pltpu.VMEM((BLK, HID), F32), pltpu.VMEM((HID, BLK), F32),
+            pltpu.VMEM((BLK, HID), BF16), pltpu.VMEM((HID, BLK), BF16),
+            pltpu.VMEM((8, 128), F32), dma(2 * SPLIT + 1), dma(2 * SPLIT),
+        ],
+        compiler_params=pltpu.CompilerParams(vmem_limit_bytes=56 * 1024 * 1024),
+        name="last_scaling",
+    )(raw_in, raw_out, factors)
     return (update_in[None], update_out[None])
 
 

time: 107 us -> 98.5 us (0.921)
  other arithmetic: 4.56 us -> 0 us
  Pallas kernels: 101 us -> 97.7 us
    pallas_call x1, Pallas kernels: 101 us -> 95.2 us  [shards(): pl.pallas_call(kernel, out_shape=(jax.ShapeDtypeStruct((BLK, HID), F32),...]
    broadcast_in_dim x2 -> x0, other arithmetic: 4.56 us -> none  [shards(): return (update_in[None], update_out[None])]
    pallas_call x0 -> x1, Pallas kernels: none -> 2.51 us  [shards(): pl.pallas_call(finish, out_shape=(jax.ShapeDtypeStruct((BLK, HID), BF16),...]
where the time goes in v4:
time: 98.5 us; the launch traced here: 98.4 us
  Pallas kernels  97.7 us (99%)
    pallas_call x1, Pallas kernels, shards(): pl.pallas_call(kernel, out_shape=(jax.ShapeDtypeStruct((BLK, HID), F32),...  95.2 us
    pallas_call x1, Pallas kernels, shards(): pl.pallas_call(finish, out_shape=(jax.ShapeDtypeStruct((BLK, HID), BF16),...  2.51 us

profile of v4, /device:TPU:1, one launch (start us, length us, event | category | flops | bytes accessed | tf_op | source)
XLA Modules:
  0.0 98.4 jit_solution(11225783393480045856)
XLA Ops:
  0.6 95.2 %switch_update.1 = (f32[512,640]{1,0:T(8,128)}, f32[640,512]{1,0:T(8,128)}, f32[8,128]{1,0:T(8,128)}) custom-call(s32[1,128]{1,0:T(1,128)} %bitcast.7, bf16[128,4096]{1,0:T(8,128)(2,1)} %tok_any.1, bf16[128,4096]{1,0:T(8,128)(2,1)} %cot_any.1, bf16[512,640]{1,0:T(8,128)(2,1)} %bitcast.5, bf16[640,512]{1,0:T(8,128)(2,1)} %bitcast.6, f32[2,8,4096]{2,1,0:T(8,128)} %ws_any.1, ...), custom_call_target="tpu_custom_call" | custom-call | tf_op jit(solution)/shard_map/switch_update/pallas_call | solution.py:656
  95.8 2.5 %last_scaling.1 = (bf16[512,640]{1,0:T(8,128)(2,1)}, bf16[640,512]{1,0:T(8,128)(2,1)}) custom-call(f32[512,640]{1,0:T(8,128)} %get-tuple-element.7.raw_in, f32[640,512]{1,0:T(8,128)} %get-tuple-element.8.raw_out, f32[8,128]{1,0:T(8,128)} %get-tuple-element.9.factors), custom_call_target="tpu_custom_call" | custom-call | tf_op jit(solution)/shard_map/last_scaling/pallas_call | solution.py:698

commit v5 on v4

--- a/solution.py
+++ b/solution.py
@@ -20,6 +20,7 @@
 PIECES = BLK // 128
 SEND = PIECES * CAP
 SPLIT = 4
+EDGE = 48
 
 DECAY_RATE = 0.9
 EPS_ONE = 1e-30
@@ -54,7 +55,7 @@
     chunk_s, chunk_r, xall, part_s, relay_r, next_r, pair_r, far_r, work, acc, slope, hp, gin, gout,
     lane_in, lane_out, stat_h, stat_w, norm_g, norm_f, factor_own,
     a2a_ss, a2a_rs, ring_ss, ring_rs, rel_ss, rel_rs, nex_ss, nex_rs, par_ss, par_rs, far_ss, far_rs, ag_ss, ag_rs,
-    sh_ss, sh_rs, sw_ss, sw_rs, ng_ss, ng_rs, nf_ss, nf_rs,
+    sh_ss, sh_rs, sw_ss, sw_rs, norm_ss, norm_rs,
     load_sem, save_sem,
 ):
     p = lax.axis_index("expert")
@@ -257,7 +258,9 @@
             met, other = pl.ds(h * half, half), pl.ds((1 - h) * half, half)
             part_s[a, m, other] = work[h, other].astype(BF16)
             part_s[a, m, met] = (work[h, met] + relay_r[a, z, h].astype(F32)).astype(BF16)
-            go(along_x(a, z, h))
+            along_x(a, z, h).start()
+            if not a:
+                sent.append(along_x(a, z, h))
 
     def ring_open(a):
         go(ring(a, mine, 0, ROWS, side(2), 0))
@@ -406,8 +409,12 @@
             total[...] += add
 
     lax.fori_loop(0, ROWS // 16, activate, 0)
-    open_spread(0)
+    go(spread(0, 0, 0, half, 4, 0))
     sum_x(1, 1)
+    along_x(1, 0, 0).wait_send()
+    go(spread(0, 0, 0, ROWS, 3, 2))
+    along_x(1, 0, 1).wait_send()
+    go(spread(0, 0, 0, ROWS, 1, 1))
     sum_x(1, 0)
     along_z(1).wait_recv()
     lax.fori_loop(0, ROWS // 16, backward, 0)
@@ -418,31 +425,35 @@
     spread(0, 3, 0, ROWS, 3, 2).wait_recv()
     go(spread(0, 3, half, half, 1, 6))
     go(spread(0, 1, 0, ROWS, 4, 3))
-    go(spread(0, 3, 0, ROWS, 4, 4))
     grads(0, 1)
     grads(0, 3)
-    spread(0, 4, 0, ROWS, 4, 0).wait_recv()
-    grads(0, 4)
     pass_pair(1)
+    go(spread(0, 3, 0, ROWS, 4, 4))
+    go(spread(0, 0, half, half, 4, 9))
     pass_next(1)
     wait_far(0)
-    go(spread(0, 2, 0, ROWS, 4, 7))
+    go(spread(0, 2, EDGE, ROWS - 2 * EDGE, 4, 10))
     grads(0, 2)
     grads(1, 0, True)
     grads(1, 4)
     grads(1, 1)
     grads(1, 3)
     spread(0, 5, 0, ROWS, 4, 3).wait_recv()
+    go(spread(0, 5, 0, EDGE, 3, 7))
     grads(0, 5)
     pass_pair_next(1)
+    spread(0, 7, 0, ROWS, 4, 4).wait_recv()
+    go(spread(0, 7, ROWS - EDGE, EDGE, 1, 8))
     grads(1, 5)
     grads(1, 7)
-    spread(0, 7, 0, ROWS, 4, 4).wait_recv()
     grads(0, 7)
+    spread(0, 4, 0, half, 4, 0).wait_recv()
+    spread(0, 4, half, half, 4, 9).wait_recv()
+    grads(0, 4)
     wait_far(1)
     grads(1, 2)
-    spread(0, 6, 0, ROWS, 4, 7).wait_recv()
-    grads(0, 6)
+    wait_pair_far(1)
+    grads(1, 6)
 
     def squares(ref, lanes, width, rows):
         def step(block, total):
@@ -462,23 +473,21 @@
     hidden_prev = hs_ref[:, pl.ds(e, 1), :]
     width_prev = ws_ref[:, pl.ds(e, 1), pl.ds(pl.multiple_of(i * BLK, BLK), BLK)]
 
-    def exchange(at, own, ssem, rsem, device):
-        copies = []
+    def exchange(buf, own, ssem, rsem, device):
+        starts = []
         for k in range(1, 8):
-            d = turn(own + k, 8)
-            copies.append((
+            starts.append(
                 pltpu.make_async_remote_copy(
-                    src_ref=at(own), dst_ref=at(own),
-                    send_sem=ssem(d), recv_sem=rsem(own),
-                    device_id=device(d), device_id_type=MESH,
-                ),
-                pltpu.make_async_remote_copy(
-                    src_ref=at(d), dst_ref=at(d),
-                    send_sem=ssem(d), recv_sem=rsem(d),
-                    device_id=device(d), device_id_type=MESH,
-                ),
-            ))
-        return copies
+                    src_ref=buf.at[own], dst_ref=buf.at[own], send_sem=ssem, recv_sem=rsem,
+                    device_id=device(turn(own + k, 8)), device_id_type=MESH,
+                )
+            )
+        seven = buf.at[pl.ds(0, 7)]
+        everything = pltpu.make_async_remote_copy(
+            src_ref=seven, dst_ref=seven, send_sem=ssem, recv_sem=rsem,
+            device_id=device(turn(own + 1, 8)), device_id_type=MESH,
+        )
+        return starts, everything
 
     def in_group(d):
         return (e * GROUP + d, f)
@@ -486,31 +495,39 @@
     def in_ffn(d):
         return (p, d)
 
-    def both(a):
-        return exchange(
-            lambda d: stat_h.at[a, d], i, lambda d: sh_ss.at[a, d], lambda d: sh_rs.at[a, d],
-            in_group,
-        ) + exchange(
-            lambda d: stat_w.at[a, d], f, lambda d: sw_ss.at[a, d], lambda d: sw_rs.at[a, d],
-            in_ffn,
-        )
-
-    stats = [both(0), both(1)]
-
+    exchanges = [
+        [
+            exchange(stat_h.at[a], i, sh_ss.at[a], sh_rs.at[a], in_group),
+            exchange(stat_w.at[a], f, sw_ss.at[a], sw_rs.at[a], in_ffn),
+        ]
+        for a in range(2)
+    ]
+    over_group = exchange(norm_g, i, norm_ss.at[0], norm_rs.at[0], in_group)
+    over_ffn = exchange(norm_f, f, norm_ss.at[1], norm_rs.at[1], in_ffn)
+
+    def begin(*several):
+        for starts, _ in several:
+            for start in starts:
+                start.start()
+
+    def collect(*several):
+        for _, everything in several:
+            everything.wait_recv()
+
+    cols_in, rows_in = squares(gin, lane_in, HID, BLK)
+    stat_h[1, i] = cols_in
+    stat_w[1, f] = jnp.concatenate([rows_in, jnp.zeros((1, 128), F32)], axis=1)
+    begin(*exchanges[1])
+
+    spread(0, 6, 0, EDGE, 3, 7).wait_recv()
+    spread(0, 6, EDGE, ROWS - 2 * EDGE, 4, 10).wait_recv()
+    spread(0, 6, ROWS - EDGE, EDGE, 1, 8).wait_recv()
+    grads(0, 6)
     cols_out, rows_out = squares(gout, lane_out, BLK, HID)
     hidden_sum = jnp.sum(hidden_prev[1], axis=1, keepdims=True)
-    stat_h[0, i] = jnp.broadcast_to(rows_out, (8, HID))
-    stat_w[0, f] = jnp.concatenate([cols_out, jnp.broadcast_to(hidden_sum, (7, BLK))], axis=0)
-    for start, _ in stats[0]:
-        start.start()
-
-    wait_pair_far(1)
-    grads(1, 6)
-    cols_in, rows_in = squares(gin, lane_in, HID, BLK)
-    stat_h[1, i] = jnp.broadcast_to(cols_in, (8, HID))
-    stat_w[1, f] = jnp.broadcast_to(rows_in, (8, BLK))
-    for start, _ in stats[1]:
-        start.start()
+    stat_h[0, i] = rows_out
+    stat_w[0, f] = jnp.concatenate([cols_out, jnp.broadcast_to(hidden_sum, (1, 128))], axis=1)
+    begin(*exchanges[0])
 
     def scaled(ref, lanes, scale, width, rows):
         def step(block, total):
@@ -526,29 +543,24 @@
         total = lax.fori_loop(0, rows // 64, step, jnp.zeros((8, 128), F32))
         return jnp.sum(total, axis=0, keepdims=True)
 
-    for _, arrival in stats[0]:
-        arrival.wait_recv()
-    sum_out = jnp.sum(stat_w[0], axis=0)
-    rows_out = DECAY_RATE * hidden_prev[1] + (1.0 - DECAY_RATE) * (
-        jnp.sum(stat_h[0], axis=0)[0:1] / D
-    )
-    cols_out = DECAY_RATE * width_prev[1] + (1.0 - DECAY_RATE) * sum_out[0:1] / FF
+    collect(*exchanges[1])
+    sum_in = jnp.sum(stat_w[1], axis=0)[:, :BLK]
+    cols_in = DECAY_RATE * hidden_prev[0] + (1.0 - DECAY_RATE) * (jnp.sum(stat_h[1], axis=0) / D)
+    rows_in = DECAY_RATE * width_prev[0] + (1.0 - DECAY_RATE) * sum_in / FF
+    lane_in[...] = jnp.broadcast_to(lax.rsqrt(rows_in), (128, BLK)).T
+    norm_in = scaled(gin, lane_in, lax.rsqrt(cols_in), HID, BLK)
+    save_in = pltpu.make_async_copy(gin, raw_in, save_sem.at[1])
+    save_in.start()
+
+    collect(*exchanges[0])
+    all_out = jnp.sum(stat_w[0], axis=0)
+    sum_out = all_out[:, :BLK]
+    rows_out = DECAY_RATE * hidden_prev[1] + (1.0 - DECAY_RATE) * (jnp.sum(stat_h[0], axis=0) / D)
+    cols_out = DECAY_RATE * width_prev[1] + (1.0 - DECAY_RATE) * sum_out / FF
     lane_out[...] = jnp.broadcast_to(lax.rsqrt(rows_out), (128, HID)).T
     norm_out = scaled(gout, lane_out, lax.rsqrt(cols_out), BLK, HID)
     save_out = pltpu.make_async_copy(gout, raw_out, save_sem.at[0])
     save_out.start()
-
-    for _, arrival in stats[1]:
-        arrival.wait_recv()
-    sum_in = jnp.sum(stat_w[1], axis=0)
-    cols_in = DECAY_RATE * hidden_prev[0] + (1.0 - DECAY_RATE) * (
-        jnp.sum(stat_h[1], axis=0)[0:1] / D
-    )
-    rows_in = DECAY_RATE * width_prev[0] + (1.0 - DECAY_RATE) * sum_in[0:1] / FF
-    lane_in[...] = jnp.broadcast_to(lax.rsqrt(rows_in), (128, BLK)).T
-    norm_in = scaled(gin, lane_in, lax.rsqrt(cols_in), HID, BLK)
-    save_in = pltpu.make_async_copy(gin, raw_in, save_sem.at[1])
-    save_in.start()
 
     def fold(row):
         total = row[:, :128]
@@ -556,41 +568,32 @@
             total = total + row[:, g * 128 : (g + 1) * 128]
         return total
 
-    norm_g[i] = jnp.concatenate(
-        [norm_in, norm_out, fold(sum_in[0:1]), fold(sum_out[0:1]), jnp.zeros((4, 128), F32)], axis=0
-    )
-    group_norms = exchange(
-        lambda d: norm_g.at[d], i, lambda d: ng_ss.at[d], lambda d: ng_rs.at[d], in_group
-    )
-    for start, _ in group_norms:
-        start.start()
-    for _, arrival in group_norms:
-        arrival.wait_recv()
+    norm_g[i] = jnp.concatenate([norm_in, norm_out, fold(sum_in), fold(sum_out)], axis=1)
+    begin(over_group)
+    collect(over_group)
     group_sum = jnp.sum(norm_g[...], axis=0)
     norm_f[f] = group_sum
-    ffn_norms = exchange(
-        lambda d: norm_f.at[d], f, lambda d: nf_ss.at[d], lambda d: nf_rs.at[d], in_ffn
-    )
-    for start, _ in ffn_norms:
-        start.start()
-    for _, arrival in ffn_norms:
-        arrival.wait_recv()
-    norm_sum = jnp.sum(jnp.sum(norm_f[...], axis=0), axis=1, keepdims=True)
-    totals = jnp.sum(group_sum, axis=1, keepdims=True)
+    begin(over_ffn)
+    collect(over_ffn)
+    norm_sum = jnp.sum(norm_f[...], axis=0)
+
+    def total(row, part):
+        return jnp.sum(row[:, part * 128 : (part + 1) * 128], axis=1, keepdims=True)
 
     whole_count = float(D) * float(FF)
     width_mean = jnp.sum(ws_ref[0, pl.ds(e, 1), :], axis=1, keepdims=True) / D
-    mean_in = DECAY_RATE * width_mean + (1.0 - DECAY_RATE) * totals[2:3] / whole_count
+    mean_in = DECAY_RATE * width_mean + (1.0 - DECAY_RATE) * total(group_sum, 2) / whole_count
     mean_out = (
-        DECAY_RATE * sum_out[1:2, 0:1] / FF + (1.0 - DECAY_RATE) * totals[3:4] / whole_count
+        DECAY_RATE * all_out[:, BLK : BLK + 1] / FF
+        + (1.0 - DECAY_RATE) * total(group_sum, 3) / whole_count
     )
     def last_factor(mean, norm):
         return jnp.sqrt(mean) / jnp.maximum(1.0, jnp.sqrt(mean * (norm / whole_count)))
 
     factor_own[...] = jnp.concatenate(
         [
-            jnp.broadcast_to(last_factor(mean_in, norm_sum[0:1]), (4, 128)),
-            jnp.broadcast_to(last_factor(mean_out, norm_sum[1:2]), (4, 128)),
+            jnp.broadcast_to(last_factor(mean_in, total(norm_sum, 0)), (4, 128)),
+            jnp.broadcast_to(last_factor(mean_out, total(norm_sum, 1)), (4, 128)),
         ],
         axis=0,
     )
@@ -610,8 +613,8 @@
 
     for copy in sent:
         copy.wait_send()
-    for start, _ in stats[0] + stats[1] + group_norms + ffn_norms:
-        start.wait_send()
+    for _, everything in exchanges[0] + exchanges[1] + [over_group, over_ffn]:
+        everything.wait_send()
 
 
 def finish(
@@ -680,14 +683,14 @@
             pltpu.VMEM((HID, BLK), F32),
             pltpu.VMEM((BLK, 128), F32),
             pltpu.VMEM((HID, 128), F32),
-            pltpu.VMEM((2, GROUP, 8, HID), F32),
-            pltpu.VMEM((2, FFN, 8, BLK), F32),
-            pltpu.VMEM((GROUP, 8, 128), F32),
-            pltpu.VMEM((FFN, 8, 128), F32),
+            pltpu.VMEM((2, GROUP, 1, HID), F32),
+            pltpu.VMEM((2, FFN, 1, BLK + 128), F32),
+            pltpu.VMEM((GROUP, 1, 512), F32),
+            pltpu.VMEM((FFN, 1, 512), F32),
             pltpu.VMEM((8, 128), F32),
             dma(2, 8), dma(2, 8), dma(2, 9), dma(2, 9), dma(2, 4), dma(2, 4), dma(2, 4),
-            dma(2, 4), dma(2), dma(2), dma(1), dma(1), dma(2, 9), dma(2, 9),
-            dma(2, 8), dma(2, 8), dma(2, 8), dma(2, 8), dma(8), dma(8), dma(8), dma(8),
+            dma(2, 4), dma(2), dma(2), dma(1), dma(1), dma(2, 11), dma(2, 11),
+            dma(2), dma(2), dma(2), dma(2), dma(2), dma(2),
             dma(7), dma(3),
         ],
         compiler_params=pltpu.CompilerParams(

time: 98.5 us -> 95.8 us (0.973)
  Pallas kernels: 97.7 us -> 95 us
    pallas_call x1, Pallas kernels: 95.2 us -> 92.5 us  [shards(): pl.pallas_call(kernel, out_shape=(jax.ShapeDtypeStruct((BLK, HID), F32),...]
where the time goes in v5:
time: 95.8 us; the launch traced here: 95.6 us
  Pallas kernels  95 us (99%)
    pallas_call x1, Pallas kernels, shards(): pl.pallas_call(kernel, out_shape=(jax.ShapeDtypeStruct((BLK, HID), F32),...  92.5 us
    pallas_call x1, Pallas kernels, shards(): pl.pallas_call(finish, out_shape=(jax.ShapeDtypeStruct((BLK, HID), BF16),...  2.51 us

profile of v5, /device:TPU:1, one launch (start us, length us, event | category | flops | bytes accessed | tf_op | source)
XLA Modules:
  0.0 95.6 jit_solution(3539346947492523623)
XLA Ops:
  0.6 92.5 %switch_update.1 = (f32[512,640]{1,0:T(8,128)}, f32[640,512]{1,0:T(8,128)}, f32[8,128]{1,0:T(8,128)}) custom-call(s32[1,128]{1,0:T(1,128)} %bitcast.7, bf16[128,4096]{1,0:T(8,128)(2,1)} %tok_any.1, bf16[128,4096]{1,0:T(8,128)(2,1)} %cot_any.1, bf16[512,640]{1,0:T(8,128)(2,1)} %bitcast.5, bf16[640,512]{1,0:T(8,128)(2,1)} %bitcast.6, f32[2,8,4096]{2,1,0:T(8,128)} %ws_any.1, ...), custom_call_target="tpu_custom_call" | custom-call | tf_op jit(solution)/shard_map/switch_update/pallas_call | solution.py:659
  93.1 2.5 %last_scaling.1 = (bf16[512,640]{1,0:T(8,128)(2,1)}, bf16[640,512]{1,0:T(8,128)(2,1)}) custom-call(f32[512,640]{1,0:T(8,128)} %get-tuple-element.7.raw_in, f32[640,512]{1,0:T(8,128)} %get-tuple-element.8.raw_out, f32[8,128]{1,0:T(8,128)} %get-tuple-element.9.factors), custom_call_target="tpu_custom_call" | custom-call | tf_op jit(solution)/shard_map/last_scaling/pallas_call | solution.py:701

commit v6 on v5

--- a/solution.py
+++ b/solution.py
@@ -102,6 +102,8 @@
             (wout_any, wout_ref), (ws_any, ws_ref), (hs_any, hs_ref),
         ))
     ]
+    loads[0].start()
+    loads[1].start()
     barrier = pltpu.get_barrier_semaphore()
     for q in range(EXPERTS):
         source = q * GROUP + mine
@@ -116,7 +118,7 @@
         )
         pl.semaphore_signal(barrier, inc=1, device_id=(p, turn(f + k, FFN)), device_id_type=MESH)
 
-    for load in loads:
+    for load in loads[2:]:
         load.start()
 
     loads[0].wait()
@@ -133,7 +135,7 @@
         target = expert * GROUP + xor(turned, expert, i)
         copy = pltpu.make_async_remote_copy(
             src_ref=chunk_s.at[a, expert], dst_ref=chunk_r.at[a, e],
-            send_sem=a2a_ss.at[a, expert], recv_sem=a2a_rs.at[a, e],
+            send_sem=a2a_ss.at[a], recv_sem=a2a_rs.at[a],
             device_id=(target, f), device_id_type=MESH,
         )
         return target, copy
@@ -170,15 +172,22 @@
                 send(a, expert - 1)
         send(a, EXPERTS - 1)
 
+    def all_routed(a, count):
+        chunks = pl.ds(0, count)
+        return pltpu.make_async_remote_copy(
+            src_ref=chunk_s.at[a, chunks], dst_ref=chunk_r.at[a, chunks],
+            send_sem=a2a_ss.at[a], recv_sem=a2a_rs.at[a],
+            device_id=place(1), device_id_type=MESH,
+        )
+
     def arrived(a):
-        for q in range(EXPERTS):
-            @pl.when(q * GROUP + mine != p)
-            def _():
-                pltpu.make_async_remote_copy(
-                    src_ref=chunk_s.at[a, q], dst_ref=chunk_r.at[a, q],
-                    send_sem=a2a_ss.at[a, q], recv_sem=a2a_rs.at[a, q],
-                    device_id=(p, f), device_id_type=MESH,
-                ).wait_recv()
+        @pl.when(mine == i)
+        def _():
+            all_routed(a, EXPERTS - 1).wait_recv()
+
+        @pl.when(mine != i)
+        def _():
+            all_routed(a, EXPERTS).wait_recv()
 
     def unpack(a):
         received = chunk_r[a].reshape(EXPERTS * SEND, 128)
@@ -195,12 +204,15 @@
         rows = pl.ds(start, size)
         return pltpu.make_async_remote_copy(
             src_ref=xall.at[a, chunk, rows], dst_ref=xall.at[a, chunk, rows],
-            send_sem=ring_ss.at[a, index], recv_sem=ring_rs.at[a, index],
+            send_sem=ring_ss.at[a], recv_sem=ring_rs.at[a, index],
             device_id=device, device_id_type=MESH,
         )
 
     half = ROWS // 2
     sent = []
+
+    def begin_copy(copy):
+        copy.start()
 
     def go(copy):
         copy.start()
@@ -263,23 +275,23 @@
                 sent.append(along_x(a, z, h))
 
     def ring_open(a):
-        go(ring(a, mine, 0, ROWS, side(2), 0))
-        go(ring(a, mine, 0, ROWS, side(6), 1))
-        go(ring(a, mine, 0, ROWS, side(1), 2))
+        begin_copy(ring(a, mine, 0, ROWS, side(2), 0))
+        begin_copy(ring(a, mine, 0, ROWS, side(6), 1))
+        begin_copy(ring(a, mine, 0, ROWS, side(1), 2))
 
     def ring_pass(a):
         ring(a, over(2), 0, ROWS, side(2), 0).wait_recv()
-        go(ring(a, over(2), 0, half, side(6), 3))
-        go(ring(a, over(2), 0, ROWS, side(1), 5))
+        begin_copy(ring(a, over(2), 0, half, side(6), 3))
+        begin_copy(ring(a, over(2), 0, ROWS, side(1), 5))
         ring(a, over(6), 0, ROWS, side(6), 1).wait_recv()
-        go(ring(a, over(6), half, half, side(2), 4))
-        go(ring(a, over(6), 0, ROWS, side(1), 6))
+        begin_copy(ring(a, over(6), half, half, side(2), 4))
+        begin_copy(ring(a, over(6), 0, ROWS, side(1), 6))
 
     def ring_halves(a):
         ring(a, over(4), 0, half, side(6), 3).wait_recv()
-        go(ring(a, over(4), 0, half, side(1), 7))
+        begin_copy(ring(a, over(4), 0, half, side(1), 7))
         ring(a, over(4), half, half, side(2), 4).wait_recv()
-        go(ring(a, over(4), half, half, side(1), 8))
+        begin_copy(ring(a, over(4), half, half, side(1), 8))
 
     def far_pair(a):
         ring(a, over(1), 0, ROWS, side(1), 2).wait_recv()
@@ -359,25 +371,25 @@
         rows = pl.ds(start, size)
         return pltpu.make_async_remote_copy(
             src_ref=hp.at[a, label(m), rows], dst_ref=hp.at[a, label(m), rows],
-            send_sem=ag_ss.at[a, index], recv_sem=ag_rs.at[a, index],
+            send_sem=ag_ss.at[a], recv_sem=ag_rs.at[a, index],
             device_id=place(to), device_id_type=MESH,
         )
 
     def open_spread(a):
-        go(spread(a, 0, 0, ROWS, 4, 0))
-        go(spread(a, 0, 0, ROWS, 1, 1))
-        go(spread(a, 0, 0, ROWS, 3, 2))
+        begin_copy(spread(a, 0, 0, ROWS, 4, 0))
+        begin_copy(spread(a, 0, 0, ROWS, 1, 1))
+        begin_copy(spread(a, 0, 0, ROWS, 3, 2))
 
     def pass_pair(a):
         spread(a, 4, 0, ROWS, 4, 0).wait_recv()
-        go(spread(a, 4, 0, ROWS, 1, 3))
-        go(spread(a, 4, 0, ROWS, 3, 4))
+        begin_copy(spread(a, 4, 0, ROWS, 1, 3))
+        begin_copy(spread(a, 4, 0, ROWS, 3, 4))
 
     def pass_next(a):
         spread(a, 1, 0, ROWS, 1, 1).wait_recv()
-        go(spread(a, 1, 0, half, 3, 5))
+        begin_copy(spread(a, 1, 0, half, 3, 5))
         spread(a, 3, 0, ROWS, 3, 2).wait_recv()
-        go(spread(a, 3, half, half, 1, 6))
+        begin_copy(spread(a, 3, half, half, 1, 6))
 
     def wait_far(a):
         spread(a, 2, 0, half, 3, 5).wait_recv()
@@ -385,9 +397,9 @@
 
     def pass_pair_next(a):
         spread(a, 5, 0, ROWS, 1, 3).wait_recv()
-        go(spread(a, 5, 0, half, 3, 7))
+        begin_copy(spread(a, 5, 0, half, 3, 7))
         spread(a, 7, 0, ROWS, 3, 4).wait_recv()
-        go(spread(a, 7, half, half, 1, 8))
+        begin_copy(spread(a, 7, half, half, 1, 8))
 
     def wait_pair_far(a):
         spread(a, 6, 0, half, 3, 7).wait_recv()
@@ -409,41 +421,41 @@
             total[...] += add
 
     lax.fori_loop(0, ROWS // 16, activate, 0)
-    go(spread(0, 0, 0, half, 4, 0))
+    begin_copy(spread(0, 0, 0, half, 4, 0))
     sum_x(1, 1)
     along_x(1, 0, 0).wait_send()
-    go(spread(0, 0, 0, ROWS, 3, 2))
+    begin_copy(spread(0, 0, 0, ROWS, 3, 2))
     along_x(1, 0, 1).wait_send()
-    go(spread(0, 0, 0, ROWS, 1, 1))
+    begin_copy(spread(0, 0, 0, ROWS, 1, 1))
     sum_x(1, 0)
     along_z(1).wait_recv()
     lax.fori_loop(0, ROWS // 16, backward, 0)
     open_spread(1)
     grads(0, 0, True)
     spread(0, 1, 0, ROWS, 1, 1).wait_recv()
-    go(spread(0, 1, 0, half, 3, 5))
+    begin_copy(spread(0, 1, 0, half, 3, 5))
     spread(0, 3, 0, ROWS, 3, 2).wait_recv()
-    go(spread(0, 3, half, half, 1, 6))
-    go(spread(0, 1, 0, ROWS, 4, 3))
+    begin_copy(spread(0, 3, half, half, 1, 6))
+    begin_copy(spread(0, 1, 0, ROWS, 4, 3))
     grads(0, 1)
     grads(0, 3)
     pass_pair(1)
-    go(spread(0, 3, 0, ROWS, 4, 4))
-    go(spread(0, 0, half, half, 4, 9))
+    begin_copy(spread(0, 3, 0, ROWS, 4, 4))
+    begin_copy(spread(0, 0, half, half, 4, 9))
     pass_next(1)
     wait_far(0)
-    go(spread(0, 2, EDGE, ROWS - 2 * EDGE, 4, 10))
+    begin_copy(spread(0, 2, EDGE, ROWS - 2 * EDGE, 4, 10))
     grads(0, 2)
     grads(1, 0, True)
     grads(1, 4)
     grads(1, 1)
     grads(1, 3)
     spread(0, 5, 0, ROWS, 4, 3).wait_recv()
-    go(spread(0, 5, 0, EDGE, 3, 7))
+    begin_copy(spread(0, 5, 0, EDGE, 3, 7))
     grads(0, 5)
     pass_pair_next(1)
     spread(0, 7, 0, ROWS, 4, 4).wait_recv()
-    go(spread(0, 7, ROWS - EDGE, EDGE, 1, 8))
+    begin_copy(spread(0, 7, ROWS - EDGE, EDGE, 1, 8))
     grads(1, 5)
     grads(1, 7)
     grads(0, 7)
@@ -603,13 +615,26 @@
     save_in.wait()
     save_out.wait()
     save_factors.wait()
+    seven = pl.ds(0, GROUP - 1)
     for a in range(2):
-        for q in range(EXPERTS):
-            target, copy = routed(a, q)
-
-            @pl.when(target != p)
-            def _():
-                copy.wait_send()
+        @pl.when(mine == i)
+        def _():
+            all_routed(a, EXPERTS - 1).wait_send()
+
+        @pl.when(mine != i)
+        def _():
+            all_routed(a, EXPERTS).wait_send()
+
+        pltpu.make_async_remote_copy(
+            src_ref=xall.at[a, seven], dst_ref=xall.at[a, seven],
+            send_sem=ring_ss.at[a], recv_sem=ring_rs.at[a, 0],
+            device_id=side(1), device_id_type=MESH,
+        ).wait_send()
+        pltpu.make_async_remote_copy(
+            src_ref=hp.at[a, seven], dst_ref=hp.at[a, seven],
+            send_sem=ag_ss.at[a], recv_sem=ag_rs.at[a, 0],
+            device_id=place(1), device_id_type=MESH,
+        ).wait_send()
 
     for copy in sent:
         copy.wait_send()
@@ -688,8 +713,8 @@
             pltpu.VMEM((GROUP, 1, 512), F32),
             pltpu.VMEM((FFN, 1, 512), F32),
             pltpu.VMEM((8, 128), F32),
-            dma(2, 8), dma(2, 8), dma(2, 9), dma(2, 9), dma(2, 4), dma(2, 4), dma(2, 4),
-            dma(2, 4), dma(2), dma(2), dma(1), dma(1), dma(2, 11), dma(2, 11),
+            dma(2), dma(2), dma(2), dma(2, 9), dma(2, 4), dma(2, 4), dma(2, 4),
+            dma(2, 4), dma(2), dma(2), dma(1), dma(1), dma(2), dma(2, 11),
             dma(2), dma(2), dma(2), dma(2), dma(2), dma(2),
             dma(7), dma(3),
         ],

time: 95.8 us -> 95.1 us (level)
  no operation moved by 1% of the time
where the time goes in v6:
time: 95.1 us; the launch traced here: 94.9 us
  Pallas kernels  94.3 us (99%)
    pallas_call x1, Pallas kernels, shards(): pl.pallas_call(kernel, out_shape=(jax.ShapeDtypeStruct((BLK, HID), F32),...  91.8 us
    pallas_call x1, Pallas kernels, shards(): pl.pallas_call(finish, out_shape=(jax.ShapeDtypeStruct((BLK, HID), BF16),...  2.51 us

profile of v6, /device:TPU:1, one launch (start us, length us, event | category | flops | bytes accessed | tf_op | source)
XLA Modules:
  0.0 94.9 jit_solution(296037346902094676)
XLA Ops:
  0.6 91.8 %switch_update.1 = (f32[512,640]{1,0:T(8,128)}, f32[640,512]{1,0:T(8,128)}, f32[8,128]{1,0:T(8,128)}) custom-call(s32[1,128]{1,0:T(1,128)} %bitcast.7, bf16[128,4096]{1,0:T(8,128)(2,1)} %tok_any.1, bf16[128,4096]{1,0:T(8,128)(2,1)} %cot_any.1, bf16[512,640]{1,0:T(8,128)(2,1)} %bitcast.5, bf16[640,512]{1,0:T(8,128)(2,1)} %bitcast.6, f32[2,8,4096]{2,1,0:T(8,128)} %ws_any.1, ...), custom_call_target="tpu_custom_call" | custom-call | tf_op jit(solution)/shard_map/switch_update/pallas_call | solution.py:684
  92.4 2.5 %last_scaling.1 = (bf16[512,640]{1,0:T(8,128)(2,1)}, bf16[640,512]{1,0:T(8,128)(2,1)}) custom-call(f32[512,640]{1,0:T(8,128)} %get-tuple-element.7.raw_in, f32[640,512]{1,0:T(8,128)} %get-tuple-element.8.raw_out, f32[8,128]{1,0:T(8,128)} %get-tuple-element.9.factors), custom_call_target="tpu_custom_call" | custom-call | tf_op jit(solution)/shard_map/last_scaling/pallas_call | solution.py:726
